TPU v7x, 32 devices: a whole 2x2x4 slice. The times are simulated.
32 devices in a mesh: tm: 4 (over z), map: 8 (over y, x, core).
Axes of the slice: x: 2, y: 2, z: 4, core: 2. Of those that a mesh axis runs over, the one named last changes fastest.
Arguments:
- points: float32 [3, 32768, 128], P(None, ('tm', 'map')), may hold values from -6 to 6
- poses: float32 [6, 1024], P(None, ('tm', 'map')), may hold values from -1.5 to 1.5
- normal_angles: float32 [2, 8192], P(None, ('tm', 'map')), may hold values from -3.140625 to 3.140625
- voxel_ids: int32 [32768], P(('tm', 'map')), may hold values from -1 to 8191, as said below
- scan_ids: int32 [32768], P(('tm', 'map')), may hold values from 0 to 255
Outputs:
- hessian: float32 [36, 1024], P(None, ('tm', 'map'))
- gradient: float32 [6, 1024], P(None, ('tm', 'map'))
- plane_cost: float32 [8192], P(('tm', 'map'))
Inputs may be any that keep to these rules, and one draw needn't show every extreme that they name: `voxel_ids`: -1 marks an empty slot. Otherwise the block at position s among the 1024 blocks of its device has its voxel among those of owner o = s // 32, that is, in [o * 256, (o + 1) * 256), where owners are devices in tm+map order. In every draw some owner gets a live block in every slot from every device.
All inputs are finite; a program needn't handle non-finite values.
Results may differ from a plain program's by a relative error of at most 0.0003.
Values sent between devices are 32-bit elements; how exact they have to be, the bound alone decides.
A program may use at most 128 MiB of HBM per device.

v0:
```python
import functools

import jax
import jax.numpy as jnp
from jax import lax
from jax.experimental import pallas as pl
from jax.experimental.pallas import tpu as pltpu
from jax.sharding import PartitionSpec as P

LANES = 128
MESH = pl.DeviceIdType.MESH
PAIRS = [(0, 0), (1, 1), (2, 2), (0, 1), (0, 2), (1, 2)]
PAIR_ROW = {}
for _k, (_i, _j) in enumerate(PAIRS):
    PAIR_ROW[(_i, _j)] = _k
    PAIR_ROW[(_j, _i)] = _k


ROWS = [("h", i, j) for i in range(6) for j in range(i, 6)] + [("g", i) for i in range(6)]


def parts_of(x):
    high = x.astype(jnp.bfloat16)
    rest = x - high.astype(jnp.float32)
    mid = rest.astype(jnp.bfloat16)
    low = (rest - mid.astype(jnp.float32)).astype(jnp.bfloat16)
    return jnp.concatenate([high, mid, low], axis=0)


def joined(y):
    rows = y.shape[0] // 3
    return y[:rows] + y[rows : 2 * rows] + y[2 * rows :]


def group_turn(pieces, out_group, group, lanes_per):
    total = None
    for a, piece in enumerate(pieces):
        shift = lax.rem((a - out_group) * lanes_per + LANES, LANES)
        if isinstance(out_group, int):
            shift = ((a - out_group) * lanes_per) % LANES
        moved = piece if isinstance(shift, int) and shift == 0 else pltpu.roll(piece, shift, 1)
        total = moved if total is None else jnp.where(group == a, moved, total)
    return total


def loop(count, body):
    if count <= 8:
        for i in range(count):
            body(i)
    else:
        def step(i, carry):
            body(i)
            return carry

        lax.fori_loop(0, count, step, 0)


def kernel(
    sizes,
    points,
    poses,
    angles,
    voxel_ids,
    scan_ids,
    packed,
    pts,
    pose_pad,
    table,
    sent,
    world,
    vox_row,
    send1,
    recv1,
    moved,
    send2,
    recv2,
    back,
    terms,
    send3,
    recv3,
    pts_sem,
    sends,
    recvs,
):
    n_tm, n_map, slots, npoints, scale = sizes
    devices = n_tm * n_map
    blocks = pts.shape[1]
    chunks = blocks // LANES
    per = LANES // slots
    own_scans = poses.shape[1]
    spread = LANES // own_scans
    scans = own_scans * n_map
    wide = scans // LANES
    voxels = angles.shape[1]
    tm = lax.axis_index("tm")
    mp = lax.axis_index("map")
    me = tm * n_map + mp

    def place(q):
        return (q // n_map, lax.rem(q, n_map))

    def chunk_copy(r):
        rows = pl.ds(r * LANES, LANES)
        return pltpu.make_async_copy(points.at[:, rows, :], pts.at[:, rows, :], pts_sem.at[r])

    loop(chunks, lambda r: chunk_copy(r).start())
    barrier = pltpu.get_barrier_semaphore()

    def greet(i, carry):
        pl.semaphore_signal(
            barrier, inc=1, device_id=place(lax.rem(me + i, devices)), device_id_type=MESH
        )
        return carry

    lax.fori_loop(1, devices, greet, 0)

    lane = lax.broadcasted_iota(jnp.int32, (8, LANES), 1)

    pose_pad[...] = jnp.zeros_like(pose_pad)
    for g in range(spread):
        pose_pad[0:6, g * own_scans : (g + 1) * own_scans] = poses[...]
    pose = pose_pad[...]
    cos, sin = jnp.cos(pose), jnp.sin(pose)
    cx, cy, cz = cos[0:1], cos[1:2], cos[2:3]
    sx, sy, sz = sin[0:1], sin[1:2], sin[2:3]
    rows = [
        cz * cy,
        cz * sy * sx - sz * cx,
        cz * sy * cx + sz * sx,
        sz * cy,
        sz * sy * sx + cz * cx,
        sz * sy * cx - cz * sx,
        -sy,
        cy * sx,
        cy * cx,
        pose[3:4],
        pose[4:5],
        pose[5:6],
    ]
    sent[...] = jnp.zeros_like(sent)

    def sent_row(k):
        return 8 * (k // 6) + k % 6

    for k, row in enumerate(rows):
        sent[pl.ds(sent_row(11 + k), chunks, stride=32), :] = jnp.broadcast_to(
            row, (chunks, LANES)
        )
    ids = voxel_ids[...]
    row_of = lax.broadcasted_iota(jnp.int32, ids.shape, 0)
    lane_of = lax.broadcasted_iota(jnp.int32, ids.shape, 1)
    owner_of = row_of * per + lane_of // slots
    local_ids = jnp.where(ids >= 0, ids - owner_of * voxels, -1).astype(jnp.float32)
    sent[pl.ds(sent_row(9), chunks, stride=32), :] = local_ids
    sent[pl.ds(sent_row(10), chunks, stride=32), :] = scan_ids[...].astype(jnp.float32)

    theta, phi = angles[0:1, :], angles[1:2, :]
    sin_theta = jnp.sin(theta)
    normal = [sin_theta * jnp.cos(phi), sin_theta * jnp.sin(phi), jnp.cos(theta)]

    def raw_moments(r):
        chunk_copy(r).wait()
        at = pl.ds(r * LANES, LANES)
        xyz = [pts[i, at, :].T for i in range(3)]
        sums = [jnp.sum(x, axis=0, keepdims=True) for x in xyz]
        sums += [jnp.sum(xyz[i] * xyz[j], axis=0, keepdims=True) for i, j in PAIRS]
        for k, row in enumerate(sums):
            sent[pl.ds(r * 32 + sent_row(k), 1), :] = row

    group = lane // slots

    def pack(r):
        raw_moments(r)
        pieces = [sent[pl.ds(pl.multiple_of(r * 32 + 8 * c, 8), 8), :] for c in range(4)]
        for g in range(per):
            send1[r * per + g] = group_turn(pieces, g, group, slots)[0:6]

    loop(chunks, pack)
    pl.semaphore_wait(barrier, devices - 1)

    def map_copy(i, source, dest, s):
        peer = lax.rem(mp + i, n_map)
        return pltpu.make_async_remote_copy(
            src_ref=source(peer),
            dst_ref=dest.at[mp],
            send_sem=sends.at[s],
            recv_sem=recvs.at[s],
            device_id=(tm, peer),
            device_id_type=MESH,
        )

    def wait_bytes(ref, sem):
        pltpu.make_async_copy(ref, ref, sem).wait()

    scan_iota = lax.broadcasted_iota(jnp.int32, (scans, LANES), 0)

    def scan_hot(r):
        return jnp.where(scan_ids[pl.ds(r, 1), :] == scan_iota, 1.0, 0.0).astype(jnp.bfloat16)

    def every(ref, k, stride):
        return ref[pl.ds(k, chunks, stride=stride), :]

    def transformed(source):
        first = [every(source, sent_row(k), 32) for k in range(3)]
        second = [every(source, sent_row(3 + k), 32) for k in range(6)]
        pose_at = [every(table, sent_row(11 + k) - 8, 24) for k in range(12)]
        rot = [pose_at[3 * i : 3 * i + 3] for i in range(3)]
        shift = pose_at[9:]
        turned = [sum(rot[i][j] * first[j] for j in range(3)) for i in range(3)]
        half_turned = [
            [sum(rot[i][k] * second[PAIR_ROW[(k, j)]] for k in range(3)) for j in range(3)]
            for i in range(3)
        ]
        m1 = [turned[i] + npoints * shift[i] for i in range(3)]
        m2 = [
            sum(half_turned[i][k] * rot[j][k] for k in range(3))
            + turned[i] * shift[j]
            + shift[i] * m1[j]
            for i, j in PAIRS
        ]
        return m1, m2

    upper = tm // (n_tm // 2)

    def all_copy(i, source, dest, s):
        step = lax.rem(i, devices) // n_map
        tm_peer = (1 - upper) * (n_tm - 1 - step) + upper * step
        peer = tm_peer * n_map + lax.rem(mp + i, n_map)
        return pltpu.make_async_remote_copy(
            src_ref=source(peer),
            dst_ref=dest.at[me],
            send_sem=sends.at[s],
            recv_sem=recvs.at[s],
            device_id=place(peer),
            device_id_type=MESH,
        ), peer

    def send_all(source, dest, s):
        def start_with(i, carry):
            copy, peer = all_copy(i, source, dest, s)

            @pl.when(peer != me)
            def _():
                copy.start()

            return carry

        lax.fori_loop(0, devices, start_with, 0, unroll=4)

    send_all(lambda peer: send1.at[peer], recv1, 1)
    recv1[me] = send1[me]
    wait_bytes(recv1.at[pl.ds(0, devices - 1)], recvs.at[1])

    vox_iota = lax.broadcasted_iota(jnp.int32, (voxels, LANES), 0).astype(jnp.float32)
    zero2 = jnp.zeros((2, LANES), jnp.float32)

    def unpack(r):
        pieces = [jnp.concatenate([recv1[r * per + g], zero2], axis=0) for g in range(per)]
        for c in range(4):
            moved[pl.ds(pl.multiple_of(r * 32 + 8 * c, 8), 8), :] = group_turn(
                pieces, c, group, slots
            )

    loop(chunks, unpack)

    def vox_hot(r):
        row = moved[pl.ds(r * 32 + sent_row(9), 1), :]
        return jnp.where(row == vox_iota, 1.0, 0.0).astype(jnp.bfloat16)

    float_iota = scan_iota.astype(jnp.float32)

    def group_parts(t):
        return parts_of(
            jnp.concatenate(
                [
                    moved[pl.ds(pl.multiple_of((t * wide + h) * 32 + 8, 8), 24), :]
                    for h in range(wide)
                ],
                axis=1,
            )
        )

    def look_up(t):
        table_parts = group_parts(t)
        for h in range(wide):
            r = t * wide + h
            row = moved[pl.ds(r * 32 + sent_row(10), 1), :]
            hot = jnp.where(row == float_iota, 1.0, 0.0).astype(jnp.bfloat16)
            found = jnp.dot(table_parts, hot, preferred_element_type=jnp.float32)
            table[pl.ds(pl.multiple_of(r * 24, 8), 24), :] = joined(found)

    loop(n_tm, look_up)
    m1, m2 = transformed(moved)
    world[...] = jnp.ones_like(world)
    for k, value in enumerate(m1 + m2):
        world[pl.ds(k, chunks, stride=16), :] = value

    contract_last = (((1,), (1,)), ((), ()))
    def add_voxels(r, acc):
        values = world[pl.ds(pl.multiple_of(r * 16, 16), 16), :]
        return acc + lax.dot_general(
            parts_of(values), vox_hot(r), contract_last, preferred_element_type=jnp.float32
        )

    def summed(body, rows, columns):
        acc = jnp.zeros((rows, columns), jnp.float32)
        if chunks <= 8:
            for r in range(chunks):
                acc = body(r, acc)
            return acc
        return lax.fori_loop(0, chunks, body, acc)

    sums = joined(summed(add_voxels, 48, voxels))
    s1 = [sums[k : k + 1] for k in range(3)]
    s2 = [sums[3 + k : 4 + k] for k in range(6)]
    floor_count = jnp.maximum(sums[9:10] * npoints, 1.0)
    offset = sum(normal[i] * s1[i] for i in range(3)) / floor_count
    quadric = sum(normal[i] ** 2 * s2[i] for i in range(3)) + 2.0 * sum(
        normal[PAIRS[k][0]] * normal[PAIRS[k][1]] * s2[k] for k in range(3, 6)
    )
    cost = quadric / floor_count - offset**2
    for h in range(voxels // LANES):
        packed[8 + h : 9 + h, :] = cost[:, h * LANES : (h + 1) * LANES]
    vox_row[...] = jnp.zeros_like(vox_row)
    for k, row in enumerate(normal + [offset]):
        vox_row[k : k + 1, :] = row
    reply_parts = parts_of(vox_row[...])

    def reply(r):
        found = jnp.dot(reply_parts, vox_hot(r), preferred_element_type=jnp.float32)
        value = joined(found)
        rolled = [value] + [pltpu.roll(value, slots * a, 1) for a in range(1, per)]
        for g in range(per):
            total = jnp.zeros_like(value)
            for c in range(4):
                total = jnp.where(corner & (group == c), rolled[(c - g) % per], total)
            send2[r * per + g] = jnp.sum(total, axis=0, keepdims=True)

    corner = lax.broadcasted_iota(jnp.int32, (8, LANES), 0) == group
    loop(chunks, reply)
    send_all(lambda peer: send2.at[peer], recv2, 2)
    recv2[me] = send2[me]

    own_parts = group_parts(tm)

    def look_up_own(r):
        found = jnp.dot(own_parts, scan_hot(r), preferred_element_type=jnp.float32)
        table[pl.ds(pl.multiple_of(r * 24, 8), 24), :] = joined(found)

    loop(chunks, look_up_own)
    m1, m2 = transformed(sent)
    wait_bytes(recv2.at[pl.ds(0, devices - 1)], recvs.at[2])

    back[...] = recv2[...].reshape(devices, LANES)
    pieces = [back[pl.ds(g, chunks, stride=per), :] for g in range(per)]
    wide_group = lane_of // slots
    n = [group_turn(pieces, c, wide_group, slots) for c in range(3)]
    d = group_turn(pieces, 3, wide_group, slots)

    def skew(v):
        return [n[2] * v[1] - n[1] * v[2], n[0] * v[2] - n[2] * v[0], n[1] * v[0] - n[0] * v[1]]

    full = [[m2[PAIR_ROW[(i, j)]] for j in range(3)] for i in range(3)]
    columns = [skew([full[k][j] for k in range(3)]) for j in range(3)]
    left = [[columns[j][i] for j in range(3)] for i in range(3)]
    corner_block = [skew(left[i]) for i in range(3)]
    skew_first = skew(m1)
    found = {}
    for i in range(3):
        for j in range(3):
            if j >= i:
                found[("h", i, j)] = corner_block[i][j]
                found[("h", 3 + i, 3 + j)] = npoints * n[i] * n[j]
            found[("h", i, 3 + j)] = skew_first[i] * n[j]
    rest = n[0] * m1[0] + n[1] * m1[1] + n[2] * m1[2] - npoints * d
    for i in range(3):
        found[("g", i)] = sum(left[i][j] * n[j] for j in range(3)) - d * skew_first[i]
        found[("g", 3 + i)] = n[i] * rest
    for name, value in found.items():
        k = ROWS.index(name)
        terms[pl.ds(k, chunks, stride=32), :] = value
    for k in range(len(found), 32):
        terms[pl.ds(k, chunks, stride=32), :] = jnp.zeros_like(d)

    def add_scans(r, acc):
        values = parts_of(terms[pl.ds(pl.multiple_of(r * 32, 32), 32), :])
        return acc + lax.dot_general(
            values, scan_hot(r), contract_last, preferred_element_type=jnp.float32
        )

    per_scan = joined(summed(add_scans, 96, scans)) * scale
    scan_group = lane // own_scans
    for h in range(wide):
        pieces = [
            per_scan[8 * c : 8 * c + 8, h * LANES : (h + 1) * LANES] for c in range(4)
        ]
        for b in range(spread):
            send3[h * spread + b] = group_turn(pieces, b, scan_group, own_scans)
    for i in range(1, n_map):
        map_copy(i, lambda peer: send3.at[peer], recv3, 0).start()
    recv3[mp] = send3[mp]
    wait_bytes(recv3.at[pl.ds(0, n_map - 1)], recvs.at[0])
    total = recv3[0]
    for m in range(1, n_map):
        total = total + recv3[m]
    packed[0:8, :] = total

    wait_bytes(send1.at[pl.ds(0, devices - 1)], sends.at[1])
    wait_bytes(recv2.at[pl.ds(0, devices - 1)], sends.at[2])
    wait_bytes(send3.at[pl.ds(0, n_map - 1)], sends.at[0])


def finish(packed, hess_out, grad_out, cost_out, lines):
    own_scans = grad_out.shape[1]
    total = packed[0:8, :]
    lined = [total] + [pltpu.roll(total, LANES - own_scans * c, 1) for c in range(1, 4)]

    def row_at(name):
        k = ROWS.index(name)
        return lined[k // 8][k % 8 : k % 8 + 1]

    lines[...] = jnp.zeros_like(lines)
    for i in range(6):
        for j in range(6):
            lines[6 * i + j : 6 * i + j + 1, :] = row_at(("h", min(i, j), max(i, j)))
        grad_out[i : i + 1, :] = row_at(("g", i))[:, 0:own_scans]
    hess_out[...] = lines[...].T[0:own_scans, 0:36]
    for h in range(cost_out.shape[1] // LANES):
        cost_out[:, h * LANES : (h + 1) * LANES] = packed[8 + h : 9 + h, :]


def local(points, poses, normal_angles, voxel_ids, scan_ids):
    blocks, npoints = points.shape[1:]
    n_tm, n_map = lax.axis_size("tm"), lax.axis_size("map")
    devices = n_tm * n_map
    slots = blocks // devices
    chunks = blocks // LANES
    vox_count = normal_angles.shape[1]
    own_scans = poses.shape[1]
    assert LANES % slots == 0 and own_scans * 4 == LANES and n_map % 4 == 0
    assert npoints == LANES and slots * 4 == LANES
    scale = own_scans * devices / (blocks * devices * npoints)
    f32 = jnp.float32
    vmem = pl.BlockSpec(memory_space=pltpu.VMEM)
    extra = -(-(vox_count // LANES) // 8) * 8
    packed = pl.pallas_call(
        functools.partial(kernel, (n_tm, n_map, slots, float(npoints), scale)),
        out_shape=jax.ShapeDtypeStruct((8 + extra, LANES), f32),
        in_specs=[pl.BlockSpec(memory_space=pl.ANY)] + [vmem] * 4,
        out_specs=vmem,
        scratch_shapes=[
            pltpu.VMEM(points.shape, f32),
            pltpu.VMEM((8, LANES), f32),
            pltpu.VMEM((chunks * 24, LANES), f32),
            pltpu.VMEM((chunks * 32, LANES), f32),
            pltpu.VMEM((chunks * 16, LANES), f32),
            pltpu.VMEM((8, vox_count), f32),
            pltpu.VMEM((devices, 6, LANES), f32),
            pltpu.VMEM((devices, 6, LANES), f32),
            pltpu.VMEM((chunks * 32, LANES), f32),
            pltpu.VMEM((devices, 1, LANES), f32),
            pltpu.VMEM((devices, 1, LANES), f32),
            pltpu.VMEM((devices, LANES), f32),
            pltpu.VMEM((chunks * 32, LANES), f32),
            pltpu.VMEM((n_map, 8, LANES), f32),
            pltpu.VMEM((n_map, 8, LANES), f32),
            pltpu.SemaphoreType.DMA((chunks,)),
            pltpu.SemaphoreType.DMA((3,)),
            pltpu.SemaphoreType.DMA((3,)),
        ],
        compiler_params=pltpu.CompilerParams(collective_id=0, has_side_effects=True),
    )(
        points,
        poses,
        normal_angles,
        voxel_ids.reshape(chunks, LANES),
        scan_ids.reshape(chunks, LANES),
    )
    hess, grad, cost = pl.pallas_call(
        finish,
        out_shape=(
            jax.ShapeDtypeStruct((own_scans, 36), f32),
            jax.ShapeDtypeStruct((6, own_scans), f32),
            jax.ShapeDtypeStruct((1, vox_count), f32),
        ),
        in_specs=[vmem],
        out_specs=(vmem, vmem, vmem),
        scratch_shapes=[pltpu.VMEM((LANES, LANES), f32)],
    )(packed)
    return hess.T, grad, cost.reshape(vox_count)


def solution(mesh):
    return jax.shard_map(
        local,
        mesh=mesh,
        in_specs=(
            P(None, ("tm", "map"), None),
            P(None, ("tm", "map")),
            P(None, ("tm", "map")),
            P(("tm", "map")),
            P(("tm", "map")),
        ),
        out_specs=(P(None, ("tm", "map")), P(None, ("tm", "map")), P(("tm", "map"))),
        check_vma=False,
    )
```

profile of v0, /device:TPU:0, one launch (start us, length us, event | category | flops | bytes accessed | tf_op | source)
XLA Modules:
  0.0 23.7 jit_solution(16928661098907082103)
XLA Ops:
  0.6 21.6 %shard_map.76.packed = f32[16,128]{1,0:T(8,128)} custom-call(f32[3,1024,128]{2,1,0:T(8,128)} %points.1, f32[6,32]{1,0:T(8,128)} %poses.1, f32[2,256]{1,0:T(2,128)} %angles.1, s32[8,128]{1,0:T(8,128)} %bitcast.4, s32[8,128]{1,0:T(8,128)} %bitcast.5), custom_call_target="tpu_custom_call" | custom-call | tf_op jit(solution)/shard_map/pallas_call | solution.py:446
  22.2 1.5 %shard_map.77 = (f32[32,36]{1,0:T(8,128)}, f32[6,32]{1,0:T(8,128)}, f32[1,256]{1,0:T(1,128)}) custom-call(f32[16,128]{1,0:T(8,128)} %shard_map.76.packed), custom_call_target="tpu_custom_call" | custom-call | tf_op jit(solution)/shard_map/pallas_call | solution.py:479
where the time goes:
time: 23.9 us; the launch traced here: 23.7 us
  Pallas kernels  23 us (96%)
  between operations  0.64 us (3%)
    pallas_call x1, Pallas kernels, local(): pl.pallas_call(functools.partial(kernel, (n_tm, n_map, slots, float(npoin...  21.6 us
    pallas_call x1, Pallas kernels, local(): pl.pallas_call(finish, out_shape=(jax.ShapeDtypeStruct((own_scans, 36), f...  1.45 us

commit v1 on v0

--- a/solution.py
+++ b/solution.py
@@ -445,7 +445,7 @@
     extra = -(-(vox_count // LANES) // 8) * 8
     packed = pl.pallas_call(
         functools.partial(kernel, (n_tm, n_map, slots, float(npoints), scale)),
-        out_shape=jax.ShapeDtypeStruct((8 + extra, LANES), f32),
+        out_shape=pltpu.VMEM((8 + extra, LANES), f32),
         in_specs=[pl.BlockSpec(memory_space=pl.ANY)] + [vmem] * 4,
         out_specs=vmem,
         scratch_shapes=[
@@ -486,7 +486,7 @@
         in_specs=[vmem],
         out_specs=(vmem, vmem, vmem),
         scratch_shapes=[pltpu.VMEM((LANES, LANES), f32)],
-    )(packed)
+    )(pltpu.with_memory_space_constraint(packed, pltpu.VMEM))
     return hess.T, grad, cost.reshape(vox_count)
 
 

time: 23.9 us -> 22.6 us (0.946)
  Pallas kernels: 23 us -> 21.7 us
    pallas_call x1, Pallas kernels: 1.45 us -> 0.76 us  [local(): pl.pallas_call(finish, out_shape=(jax.ShapeDtypeStruct((own_scans, 36), f...]
    pallas_call x1, Pallas kernels: 21.6 us -> 21 us  [local(): pl.pallas_call(functools.partial(kernel, (n_tm, n_map, slots, float(npoin...]
where the time goes in v1:
time: 22.6 us; the launch traced here: 22.4 us
  Pallas kernels  21.7 us (96%)
  between operations  0.64 us (3%)
    pallas_call x1, Pallas kernels, local(): pl.pallas_call(functools.partial(kernel, (n_tm, n_map, slots, float(npoin...  21 us
    pallas_call x1, Pallas kernels, local(): pl.pallas_call(finish, out_shape=(jax.ShapeDtypeStruct((own_scans, 36), f...  0.76 us

profile of v1, /device:TPU:0, one launch (start us, length us, event | category | flops | bytes accessed | tf_op | source)
XLA Modules:
  0.0 22.4 jit_solution(6262613770003022659)
XLA Ops:
  0.6 21.0 %shard_map.76.packed = f32[16,128]{1,0:T(8,128)S(1)} custom-call(f32[3,1024,128]{2,1,0:T(8,128)} %points.1, f32[6,32]{1,0:T(8,128)} %poses.1, f32[2,256]{1,0:T(2,128)} %angles.1, s32[8,128]{1,0:T(8,128)} %bitcast.4, s32[8,128]{1,0:T(8,128)} %bitcast.5), custom_call_target="tpu_custom_call" | custom-call | tf_op jit(solution)/shard_map/pallas_call | solution.py:446
  21.6 0.8 %shard_map.77 = (f32[32,36]{1,0:T(8,128)}, f32[6,32]{1,0:T(8,128)}, f32[1,256]{1,0:T(1,128)}) custom-call(f32[16,128]{1,0:T(8,128)S(1)} %shard_map.76.packed), custom_call_target="tpu_custom_call" | custom-call | tf_op jit(solution)/shard_map/pallas_call | solution.py:479

commit v2 on v1

v2 whole, which is shorter than its diff:
```python
import functools

import jax
import jax.numpy as jnp
from jax import lax
from jax.experimental import pallas as pl
from jax.experimental.pallas import tpu as pltpu
from jax.sharding import PartitionSpec as P

LANES = 128
MESH = pl.DeviceIdType.MESH
PAIRS = [(0, 0), (1, 1), (2, 2), (0, 1), (0, 2), (1, 2)]
PAIR_ROW = {}
for _k, (_i, _j) in enumerate(PAIRS):
    PAIR_ROW[(_i, _j)] = _k
    PAIR_ROW[(_j, _i)] = _k

ROWS = [("h", i, j) for i in range(6) for j in range(i, 6)] + [("g", i) for i in range(6)]

TILE = 16
VOX_ROW, SCAN_ROW, POSE_ROW = 9, 10, 12
CONTRACT_LAST = (((1,), (1,)), ((), ()))


def split(x):
    high = x.astype(jnp.bfloat16).astype(jnp.float32)
    rest = x - high
    mid = rest.astype(jnp.bfloat16).astype(jnp.float32)
    return jnp.concatenate([high, mid, rest - mid], axis=0).astype(jnp.bfloat16)


def joined(y):
    rows = y.shape[0] // 3
    return y[:rows] + y[rows : 2 * rows] + y[2 * rows :]


def group_turn(pieces, out_group, group, lanes_per):
    total = None
    for a, piece in enumerate(pieces):
        shift = ((a - out_group) * lanes_per) % LANES
        moved = piece if shift == 0 else pltpu.roll(piece, shift, 1)
        total = moved if total is None else jnp.where(group == a, moved, total)
    return total


def loop(count, body):
    if count <= 8:
        for i in range(count):
            body(i)
    else:
        def step(i, carry):
            body(i)
            return carry

        lax.fori_loop(0, count, step, 0)


def summed(count, body, rows, columns):
    acc = jnp.zeros((rows, columns), jnp.float32)
    if count <= 8:
        for i in range(count):
            acc = acc + body(i)
        return acc
    return lax.fori_loop(0, count, lambda i, total: total + body(i), acc)


def aligned(start, size, unit=8):
    if not isinstance(start, int):
        start = pl.multiple_of(start, unit)
    return pl.ds(start, size)


def kernel(
    sizes,
    points,
    poses,
    angles,
    voxel_ids,
    scan_ids,
    hess_out,
    grad_out,
    cost_out,
    pts,
    pose_in,
    angle_in,
    vox_in,
    scan_in,
    pose_pad,
    sent,
    send1,
    recv1,
    send_n,
    recv_n,
    scan_hot,
    vox_hot,
    table,
    world,
    send_a,
    recv_a,
    total_a,
    normals,
    quads,
    send_q,
    recv_q,
    terms,
    late,
    send_h,
    recv_h,
    send_g,
    recv_g,
    lines,
    pts_sem,
    in_sem,
    sends,
    recvs,
):
    n_tm, n_map, slots, npoints, scale = sizes
    blocks = pts.shape[1]
    chunks = blocks // LANES
    per = LANES // slots
    own_scans = pose_in.shape[1]
    spread = LANES // own_scans
    scans = own_scans * n_map
    wide = scans // LANES
    voxels = angle_in.shape[1]
    halves = voxels // LANES
    parts = n_tm // per
    arrived = n_map * parts
    pairs = arrived // 2
    message = parts * TILE
    a_rows = 2 * n_tm
    tm = lax.axis_index("tm")
    mp = lax.axis_index("map")
    f32, bf16 = jnp.float32, jnp.bfloat16

    small = [
        pltpu.make_async_copy(src, dst, in_sem.at[i])
        for i, (src, dst) in enumerate(
            [(poses, pose_in), (angles, angle_in), (voxel_ids, vox_in), (scan_ids, scan_in)]
        )
    ]
    loads = pts_sem.shape[0]
    span = blocks // loads

    def points_copy(r):
        rows = pl.ds(r * span, span)
        return pltpu.make_async_copy(points.at[:, rows, :], pts.at[:, rows, :], pts_sem.at[r])

    for copy in small:
        copy.start()
    loop(loads, lambda r: points_copy(r).start())
    barrier = pltpu.get_barrier_semaphore()
    plane = [(tm, lax.rem(mp + i, n_map)) for i in range(1, n_map)]
    column = [(lax.rem(tm + i, n_tm), mp) for i in range(1, n_tm)]
    for peer in column + plane:
        pl.semaphore_signal(barrier, inc=1, device_id=peer, device_id_type=MESH)

    def send(source, dest, peer, s):
        pltpu.make_async_remote_copy(
            src_ref=source,
            dst_ref=dest,
            send_sem=sends.at[0],
            recv_sem=recvs.at[s],
            device_id=peer,
            device_id_type=MESH,
        ).start()

    def wait_rows(rows, sem):
        ref = pts.at[0, pl.ds(0, rows), :]
        pltpu.make_async_copy(ref, ref, sem).wait()

    def every(ref, k, stride, count=arrived):
        return ref[pl.ds(k, count, stride=stride), :]

    lane = lax.broadcasted_iota(jnp.int32, (8, LANES), 1)
    group = lane // slots
    chunk_of = lax.broadcasted_iota(jnp.int32, (arrived, LANES), 0)
    turn_of = (
        lax.broadcasted_iota(jnp.int32, (arrived, LANES), 1) // slots + per * lax.rem(chunk_of, parts)
    )
    own_turn = [turn_of == t for t in range(n_tm)]
    for t in range(n_tm):
        world[pl.ds(3 * n_tm + t, arrived, stride=4 * n_tm), :] = jnp.where(own_turn[t], 1.0, 0.0)
    sent[...] = jnp.zeros_like(sent)
    quads[...] = jnp.zeros_like(quads)
    late[...] = jnp.zeros_like(late)
    pose_pad[...] = jnp.zeros_like(pose_pad)
    lines[...] = jnp.zeros_like(lines)

    for copy in small:
        copy.wait()
    for g in range(spread):
        pose_pad[0:6, g * own_scans : (g + 1) * own_scans] = pose_in[...]
    pose = pose_pad[...]
    cos, sin = jnp.cos(pose), jnp.sin(pose)
    cx, cy, cz = cos[0:1], cos[1:2], cos[2:3]
    sx, sy, sz = sin[0:1], sin[1:2], sin[2:3]
    pose_rows = [
        [cz * cy, cz * sy * sx - sz * cx, cz * sy * cx + sz * sx],
        [sz * cy, sz * sy * sx + cz * cx, sz * sy * cx - cz * sx],
        [-sy, cy * sx, cy * cx],
        [pose[3:4], pose[4:5], pose[5:6]],
    ]
    scan_group = lane[0:1] // own_scans
    pose_lines = []
    for q in range(3):
        line = pose_rows[0][q]
        for g in range(1, 4):
            line = jnp.where(scan_group == g, pose_rows[g][q], line)
        pose_lines.append(line)

    ids = vox_in[...]
    row_of = lax.broadcasted_iota(jnp.int32, ids.shape, 0)
    lane_of = lax.broadcasted_iota(jnp.int32, ids.shape, 1)
    owner_of = row_of * per + lane_of // slots
    local_ids = jnp.where(ids >= 0, ids - owner_of * voxels, -1).astype(f32)
    sent[pl.ds(VOX_ROW, chunks, stride=TILE), :] = local_ids
    sent[pl.ds(SCAN_ROW, chunks, stride=TILE), :] = scan_in[...].astype(f32)

    theta, phi = angle_in[0:1, :], angle_in[1:2, :]
    sin_theta = jnp.sin(theta)
    own_normal = [sin_theta * jnp.cos(phi), sin_theta * jnp.sin(phi), jnp.cos(theta)]
    for c in range(3):
        for h in range(halves):
            k = c * halves + h
            send_n[k : k + 1, :] = own_normal[c][:, h * LANES : (h + 1) * LANES]

    def raw_moments(r):
        at = aligned(r * LANES, LANES, LANES)
        xyz = [pts[i, at, :].T for i in range(3)]
        sums = [jnp.sum(x, axis=0, keepdims=True) for x in xyz]
        sums += [jnp.sum(xyz[i] * xyz[j], axis=0, keepdims=True) for i, j in PAIRS]
        for k, row in enumerate(sums):
            sent[pl.ds(r * TILE + k, 1), :] = row

    def load_step(r):
        points_copy(r).wait()
        for i in range(span // LANES):
            raw_moments(r * (span // LANES) + i)

    loop(loads, load_step)
    row_chunks = n_map // per

    def pack(peer_row):
        for g in range(per):
            peer = peer_row * per + g
            for u in range(parts):
                for half in range(2):
                    pieces = [
                        sent[
                            aligned(
                                ((u * per + a) * row_chunks + peer_row) * TILE + 8 * half, 8
                            ),
                            :,
                        ]
                        for a in range(per)
                    ]
                    at = aligned(peer * message + u * TILE + 8 * half, 8)
                    send1[at, :] = group_turn(pieces, g, group, slots)
            for q in range(3):
                send1[pl.ds(peer * message + POSE_ROW + q, 1), :] = pose_lines[q]

    loop(row_chunks, pack)

    pl.semaphore_wait(barrier, n_map - 1 + n_tm - 1)
    mine = aligned(mp * message, message)
    for peer in plane:
        send(send1.at[aligned(peer[1] * message, message), :], recv1.at[mine, :], peer, 0)
    n_size = send_n.shape[0]
    n_mine = aligned(tm * n_size, n_size)
    for peer in column:
        send(send_n, recv_n.at[n_mine, :], peer, 1)
    recv1[mine, :] = send1[mine, :]
    recv_n[n_mine, :] = send_n[...]
    wait_rows((n_map - 1) * message, recvs.at[0])

    def pair_row(p, k):
        return jnp.concatenate(
            [recv1[pl.ds((2 * p + i) * TILE + k, 1), :] for i in range(2)], axis=1
        )

    scan_iota = lax.broadcasted_iota(jnp.int32, (scans, 2 * LANES), 0).astype(f32)
    vox_iota = lax.broadcasted_iota(jnp.int32, (voxels, 2 * LANES), 0).astype(f32)

    def mark(p):
        scan_hot[p] = jnp.where(pair_row(p, SCAN_ROW) == scan_iota, 1.0, 0.0).astype(bf16)
        vox_hot[p] = jnp.where(pair_row(p, VOX_ROW) == vox_iota, 1.0, 0.0).astype(bf16)

    top = lax.broadcasted_iota(jnp.int32, (8, LANES), 0) < 4
    columns = []
    for h in range(wide):
        tiles = [recv1[(h * spread + a) * message + 8 : (h * spread + a) * message + 16, :] for a in range(spread)]
        turned = [group_turn(tiles, g, group, own_scans) for g in range(4)]
        low = jnp.where(top, pltpu.roll(turned[1], 4, 0), turned[0])
        high = jnp.where(top, pltpu.roll(turned[3], 4, 0), turned[2])
        columns.append(jnp.concatenate([low, high], axis=0))
    pose_table = split(jnp.concatenate(columns, axis=1))
    table_row = {}
    for q in range(3):
        table_row[(1, q)], table_row[(0, q)] = q, 4 + q
        table_row[(3, q)], table_row[(2, q)] = 8 + q, 12 + q

    def look_up(p):
        mark(p)
        found = joined(jnp.dot(pose_table, scan_hot[p], preferred_element_type=f32))
        for i in range(2):
            table[aligned((2 * p + i) * TILE, TILE), :] = found[:, i * LANES : (i + 1) * LANES]

    loop(pairs, look_up)
    rot = [[every(table, table_row[(i, j)], TILE) for j in range(3)] for i in range(3)]
    shift = [every(table, table_row[(3, j)], TILE) for j in range(3)]
    first = [every(recv1, k, TILE) for k in range(3)]
    turned_first = [sum(rot[i][j] * first[j] for j in range(3)) for i in range(3)]
    m1 = [turned_first[i] + npoints * shift[i] for i in range(3)]
    for c in range(3):
        for t in range(n_tm):
            world[pl.ds(c * n_tm + t, arrived, stride=4 * n_tm), :] = jnp.where(
                own_turn[t], m1[c], 0.0
            )

    def pair_tile(ref, p, rows):
        return jnp.concatenate(
            [ref[aligned((2 * p + i) * rows, rows), :] for i in range(2)], axis=1
        )

    def add_voxels(p):
        return lax.dot_general(
            split(pair_tile(world, p, 4 * n_tm)), vox_hot[p], CONTRACT_LAST,
            preferred_element_type=f32,
        )

    sums = joined(summed(pairs, add_voxels, 12 * n_tm, voxels))
    wait_rows((n_tm - 1) * n_size, recvs.at[1])
    normal = [
        jnp.concatenate(
            [every(recv_n, c * halves + h, n_size, n_tm) for h in range(halves)], axis=1
        )
        for c in range(3)
    ]
    along = sum(normal[c] * sums[c * n_tm : (c + 1) * n_tm] for c in range(3))
    count = sums[3 * n_tm : 4 * n_tm]
    for h in range(halves):
        at = slice(h * LANES, (h + 1) * LANES)
        send_a[h * a_rows : h * a_rows + n_tm, :] = along[:, at]
        send_a[h * a_rows + n_tm : (h + 1) * a_rows, :] = count[:, at]

    a_size = halves * a_rows
    a_mine = aligned(tm * a_size, a_size)
    for peer in column:
        send(send_a, recv_a.at[a_mine, :], peer, 2)
    recv_a[a_mine, :] = send_a[...]

    normal_table = split(jnp.concatenate(normal + [jnp.zeros_like(count)], axis=0))

    def find_normals(p):
        found = joined(jnp.dot(normal_table, vox_hot[p], preferred_element_type=f32))
        for i in range(2):
            normals[aligned((2 * p + i) * 4 * n_tm, 4 * n_tm), :] = found[
                :, i * LANES : (i + 1) * LANES
            ]

    loop(pairs, find_normals)
    n = []
    for c in range(3):
        value = every(normals, c * n_tm, 4 * n_tm)
        for t in range(1, n_tm):
            value = jnp.where(own_turn[t], every(normals, c * n_tm + t, 4 * n_tm), value)
        n.append(value)
    second = [every(recv1, 3 + k, TILE) for k in range(6)]
    half_turned = [
        [sum(rot[i][k] * second[PAIR_ROW[(k, j)]] for k in range(3)) for j in range(3)]
        for i in range(3)
    ]
    m2 = [
        sum(half_turned[i][k] * rot[j][k] for k in range(3))
        + turned_first[i] * shift[j]
        + shift[i] * m1[j]
        for i, j in PAIRS
    ]
    quad = sum(n[i] ** 2 * m2[i] for i in range(3)) + 2.0 * sum(
        n[PAIRS[k][0]] * n[PAIRS[k][1]] * m2[k] for k in range(3, 6)
    )
    for t in range(n_tm):
        quads[pl.ds(t, arrived, stride=8), :] = jnp.where(own_turn[t], quad, 0.0)

    def add_quads(p):
        return lax.dot_general(
            split(pair_tile(quads, p, 8)), vox_hot[p], CONTRACT_LAST, preferred_element_type=f32
        )

    quad_sums = joined(summed(pairs, add_quads, 24, voxels))
    for t in range(n_tm):
        for h in range(halves):
            send_q[t, h : h + 1, :] = quad_sums[t : t + 1, h * LANES : (h + 1) * LANES]
    for peer in column:
        send(send_q.at[peer[0]], recv_q.at[tm], peer, 3)
    recv_q[tm] = send_q[tm]

    def skew(v):
        return [n[2] * v[1] - n[1] * v[2], n[0] * v[2] - n[2] * v[0], n[1] * v[0] - n[0] * v[1]]

    full = [[m2[PAIR_ROW[(i, j)]] for j in range(3)] for i in range(3)]
    skewed = [skew([full[k][j] for k in range(3)]) for j in range(3)]
    left = [[skewed[j][i] for j in range(3)] for i in range(3)]
    corner_block = [skew(left[i]) for i in range(3)]
    skew_first = skew(m1)
    found = {}
    for i in range(3):
        for j in range(3):
            if j >= i:
                found[("h", i, j)] = corner_block[i][j]
                found[("h", 3 + i, 3 + j)] = npoints * n[i] * n[j]
            found[("h", i, 3 + j)] = skew_first[i] * n[j]
    rest = n[0] * m1[0] + n[1] * m1[1] + n[2] * m1[2]
    for i in range(3):
        found[("g", i)] = sum(left[i][j] * n[j] for j in range(3))
        found[("g", 3 + i)] = n[i] * rest
        late[pl.ds(i, arrived, stride=8), :] = skew_first[i]
        late[pl.ds(3 + i, arrived, stride=8), :] = npoints * n[i]
    for name, value in found.items():
        terms[pl.ds(ROWS.index(name), arrived, stride=32), :] = value
    for k in range(len(found), 32):
        terms[pl.ds(k, arrived, stride=32), :] = jnp.zeros_like(rest)

    def add_scans(p):
        return lax.dot_general(
            split(pair_tile(terms, p, 32)), scan_hot[p], CONTRACT_LAST, preferred_element_type=f32
        )

    per_scan = joined(summed(pairs, add_scans, 96, scans)) * scale
    own_group = lane // own_scans
    for h in range(wide):
        pieces = [per_scan[8 * c : 8 * c + 8, h * LANES : (h + 1) * LANES] for c in range(4)]
        for b in range(spread):
            at = (h * spread + b) * 8
            send_h[at : at + 8, :] = group_turn(pieces, b, own_group, own_scans)
    eight = aligned(mp * 8, 8)
    for peer in plane:
        send(send_h.at[aligned(peer[1] * 8, 8), :], recv_h.at[eight, :], peer, 4)
    recv_h[eight, :] = send_h[eight, :]

    wait_rows((n_tm - 1) * a_size, recvs.at[2])
    offsets = []
    for h in range(halves):
        total = recv_a[h * a_rows : (h + 1) * a_rows, :]
        for t in range(1, n_tm):
            total = total + recv_a[t * a_size + h * a_rows : t * a_size + (h + 1) * a_rows, :]
        floor = jnp.maximum(total[n_tm:] * npoints, 1.0)
        offset = total[:n_tm] / floor
        total_a[h * a_rows : h * a_rows + n_tm, :] = offset
        total_a[h * a_rows + n_tm : (h + 1) * a_rows, :] = floor
        offsets.append(offset)
    offset = jnp.concatenate(offsets, axis=1)
    if n_tm % 8:
        offset = jnp.concatenate([offset, jnp.zeros((8 - n_tm % 8, voxels), f32)], axis=0)
    offset_table = split(offset)
    d_rows = offset.shape[0]
    turn_row = lax.broadcasted_iota(jnp.int32, (d_rows, 2 * LANES), 0)
    turn_lane = lax.rem(lax.broadcasted_iota(jnp.int32, (d_rows, 2 * LANES), 1), LANES) // slots

    def add_late(p):
        value = joined(jnp.dot(offset_table, vox_hot[p], preferred_element_type=f32))
        turn = turn_lane
        if parts > 1:
            in_pair = lax.broadcasted_iota(jnp.int32, (d_rows, 2 * LANES), 1) // LANES
            turn = turn_lane + per * lax.rem(2 * p + in_pair, parts)
        d = jnp.sum(jnp.where(turn_row == turn, value, 0.0), axis=0, keepdims=True)
        return lax.dot_general(
            split(pair_tile(late, p, 8) * d), scan_hot[p], CONTRACT_LAST,
            preferred_element_type=f32,
        )

    moved = joined(summed(pairs, add_late, 24, scans)) * scale
    for h in range(wide):
        send_g[h * 8 : h * 8 + 8, :] = moved[:, h * LANES : (h + 1) * LANES]
    for peer in plane:
        source = send_g.at[aligned(peer[1] // spread * 8, 8), :]
        send(source, recv_g.at[eight, :], peer, 5)
    recv_g[eight, :] = send_g[aligned(mp // spread * 8, 8), :]

    wait_rows((n_map - 1) * 8, recvs.at[4])
    total = recv_h[0:8, :]
    for m in range(1, n_map):
        total = total + recv_h[m * 8 : m * 8 + 8, :]
    lined = [total] + [pltpu.roll(total, LANES - own_scans * c, 1) for c in range(1, 4)]

    def row_at(name):
        k = ROWS.index(name)
        return lined[k // 8][k % 8 : k % 8 + 1]

    for i in range(6):
        for j in range(6):
            lines[6 * i + j : 6 * i + j + 1, :] = row_at(("h", min(i, j), max(i, j)))
    hess_out[...] = lines[...].T[0:own_scans, 0:36]
    gradient = jnp.concatenate([row_at(("g", i)) for i in range(6)], axis=0)

    pltpu.make_async_copy(
        recv_q.at[pl.ds(0, n_tm - 1)], recv_q.at[pl.ds(0, n_tm - 1)], recvs.at[3]
    ).wait()
    quad_total = recv_q[0]
    for t in range(1, n_tm):
        quad_total = quad_total + recv_q[t]
    own_offset = total_a[pl.ds(tm, halves, stride=a_rows), :]
    own_floor = total_a[pl.ds(n_tm + tm, halves, stride=a_rows), :]
    cost = quad_total / own_floor - own_offset**2
    for h in range(halves):
        cost_out[:, h * LANES : (h + 1) * LANES] = cost[h : h + 1]

    wait_rows((n_map - 1) * 8, recvs.at[5])
    change = recv_g[0:8, :]
    for m in range(1, n_map):
        change = change + recv_g[m * 8 : m * 8 + 8, :]
    change = pltpu.roll(change, LANES - own_scans * lax.rem(mp, spread), 1)
    grad_out[...] = (gradient - change[0:6])[:, 0:own_scans]

    rows_sent = (n_map - 1) * (message + 16) + (n_tm - 1) * (n_size + a_size + halves)
    wait_rows(rows_sent, sends.at[0])


def finish(hess_in, grad_in, cost_in, hess_out, grad_out, cost_out, sems):
    copies = [
        pltpu.make_async_copy(src, dst, sems.at[i])
        for i, (src, dst) in enumerate(
            [(hess_in, hess_out), (grad_in, grad_out), (cost_in, cost_out)]
        )
    ]
    for copy in copies:
        copy.start()
    for copy in copies:
        copy.wait()


def local(points, poses, normal_angles, voxel_ids, scan_ids):
    blocks, npoints = points.shape[1:]
    n_tm, n_map = lax.axis_size("tm"), lax.axis_size("map")
    devices = n_tm * n_map
    slots = blocks // devices
    chunks = blocks // LANES
    vox_count = normal_angles.shape[1]
    own_scans = poses.shape[1]
    assert npoints == LANES and slots * 4 == LANES and own_scans * 4 == LANES
    assert n_map % 4 == 0 and n_tm % 4 == 0 and vox_count % LANES == 0
    scale = own_scans * devices / (blocks * devices * npoints)
    f32, bf16 = jnp.float32, jnp.bfloat16
    scans = own_scans * n_map
    halves = vox_count // LANES
    arrived = n_map * n_tm // 4
    n_rows = -(-3 * halves // 8) * 8
    a_rows = 2 * n_tm * halves
    hbm = pl.BlockSpec(memory_space=pl.ANY)
    vmem = pl.BlockSpec(memory_space=pltpu.VMEM)
    shapes = [(own_scans, 36), (6, own_scans), (1, vox_count)]
    results = pl.pallas_call(
        functools.partial(kernel, (n_tm, n_map, slots, float(npoints), scale)),
        out_shape=tuple(pltpu.VMEM(shape, f32) for shape in shapes),
        in_specs=[hbm] * 5,
        out_specs=(vmem,) * 3,
        scratch_shapes=[
            pltpu.VMEM(points.shape, f32),
            pltpu.VMEM(poses.shape, f32),
            pltpu.VMEM(normal_angles.shape, f32),
            pltpu.VMEM((chunks, LANES), jnp.int32),
            pltpu.VMEM((chunks, LANES), jnp.int32),
            pltpu.VMEM((8, LANES), f32),
            pltpu.VMEM((chunks * TILE, LANES), f32),
            pltpu.VMEM((arrived * TILE, LANES), f32),
            pltpu.VMEM((arrived * TILE, LANES), f32),
            pltpu.VMEM((n_rows, LANES), f32),
            pltpu.VMEM((n_tm * n_rows, LANES), f32),
            pltpu.VMEM((arrived // 2, scans, 2 * LANES), bf16),
            pltpu.VMEM((arrived // 2, vox_count, 2 * LANES), bf16),
            pltpu.VMEM((arrived * TILE, LANES), f32),
            pltpu.VMEM((arrived * 4 * n_tm, LANES), f32),
            pltpu.VMEM((a_rows, LANES), f32),
            pltpu.VMEM((n_tm * a_rows, LANES), f32),
            pltpu.VMEM((a_rows, LANES), f32),
            pltpu.VMEM((arrived * 4 * n_tm, LANES), f32),
            pltpu.VMEM((arrived * 8, LANES), f32),
            pltpu.VMEM((n_tm, halves, LANES), f32),
            pltpu.VMEM((n_tm, halves, LANES), f32),
            pltpu.VMEM((arrived * 32, LANES), f32),
            pltpu.VMEM((arrived * 8, LANES), f32),
            pltpu.VMEM((n_map * 8, LANES), f32),
            pltpu.VMEM((n_map * 8, LANES), f32),
            pltpu.VMEM((scans // LANES * 8, LANES), f32),
            pltpu.VMEM((n_map * 8, LANES), f32),
            pltpu.VMEM((LANES, LANES), f32),
            pltpu.SemaphoreType.DMA((4,)),
            pltpu.SemaphoreType.DMA((4,)),
            pltpu.SemaphoreType.DMA((1,)),
            pltpu.SemaphoreType.DMA((6,)),
        ],
        compiler_params=pltpu.CompilerParams(collective_id=0, has_side_effects=True),
    )(
        points,
        poses,
        normal_angles,
        voxel_ids.reshape(chunks, LANES),
        scan_ids.reshape(chunks, LANES),
    )
    hess, grad, cost = pl.pallas_call(
        finish,
        out_shape=tuple(jax.ShapeDtypeStruct(shape, f32) for shape in shapes),
        in_specs=[vmem] * 3,
        out_specs=(hbm,) * 3,
        scratch_shapes=[pltpu.SemaphoreType.DMA((3,))],
    )(*[pltpu.with_memory_space_constraint(x, pltpu.VMEM) for x in results])
    return hess.T, grad, cost.reshape(vox_count)


def solution(mesh):
    return jax.shard_map(
        local,
        mesh=mesh,
        in_specs=(
            P(None, ("tm", "map"), None),
            P(None, ("tm", "map")),
            P(None, ("tm", "map")),
            P(("tm", "map")),
            P(("tm", "map")),
        ),
        out_specs=(P(None, ("tm", "map")), P(None, ("tm", "map")), P(("tm", "map"))),
        check_vma=False,
    )
```

time: 22.6 us -> 18.5 us (0.82)
  Pallas kernels: 21.7 us -> 17.7 us
    pallas_call x1, Pallas kernels: 21 us -> 17.1 us  [local(): pl.pallas_call(functools.partial(kernel, (n_tm, n_map, slots, float(npoin...]
where the time goes in v2:
time: 18.5 us; the launch traced here: 18.4 us
  Pallas kernels  17.7 us (96%)
  between operations  0.64 us (3%)
    pallas_call x1, Pallas kernels, local(): pl.pallas_call(functools.partial(kernel, (n_tm, n_map, slots, float(npoin...  17.1 us
    pallas_call x1, Pallas kernels, local(): pl.pallas_call(finish, out_shape=tuple((jax.ShapeDtypeStruct(shape, f32)...  0.64 us

profile of v2, /device:TPU:0, one launch (start us, length us, event | category | flops | bytes accessed | tf_op | source)
XLA Modules:
  0.0 18.4 jit_solution(5295684202580953700)
XLA Ops:
  0.6 17.1 %shard_map.76 = (f32[32,36]{1,0:T(8,128)S(1)}, f32[6,32]{1,0:T(8,128)S(1)}, f32[1,256]{1,0:T(1,128)S(1)}) custom-call(f32[3,1024,128]{2,1,0:T(8,128)} %points.1, f32[6,32]{1,0:T(8,128)} %poses.1, f32[2,256]{1,0:T(2,128)} %angles.1, s32[8,128]{1,0:T(8,128)} %bitcast.4, s32[8,128]{1,0:T(8,128)} %bitcast.5), custom_call_target="tpu_custom_call" | custom-call | tf_op jit(solution)/shard_map/pallas_call | solution.py:553
  17.7 0.6 %shard_map.77 = (f32[32,36]{1,0:T(8,128)}, f32[6,32]{1,0:T(8,128)}, f32[1,256]{1,0:T(1,128)}) custom-call(f32[32,36]{1,0:T(8,128)S(1)} %get-tuple-element.9.hess_in, f32[6,32]{1,0:T(8,128)S(1)} %get-tuple-element.10.grad_in, f32[1,256]{1,0:T(1,128)S(1)} %get-tuple-element.11.cost_in), custom_call_target="tpu_custom_call" | custom-call | tf_op jit(solution)/shard_map/pallas_call | solution.py:601

commit v3 on v2

v3 whole, which is shorter than its diff:
```python
import functools

import jax
import jax.numpy as jnp
from jax import lax
from jax.experimental import pallas as pl
from jax.experimental.pallas import tpu as pltpu
from jax.sharding import PartitionSpec as P

LANES = 128
MESH = pl.DeviceIdType.MESH
PAIRS = [(0, 0), (1, 1), (2, 2), (0, 1), (0, 2), (1, 2)]
PAIR_ROW = {}
for _k, (_i, _j) in enumerate(PAIRS):
    PAIR_ROW[(_i, _j)] = _k
    PAIR_ROW[(_j, _i)] = _k

ROWS = [("h", i, j) for i in range(6) for j in range(i, 6)] + [("g", i) for i in range(6)]

TILE = 16
VOX_ROW, SCAN_ROW, POSE_ROW = 9, 10, 12
SHARE = 2
CONTRACT_LAST = (((1,), (1,)), ((), ()))


def split(x):
    high = x.astype(jnp.bfloat16).astype(jnp.float32)
    rest = x - high
    mid = rest.astype(jnp.bfloat16).astype(jnp.float32)
    return jnp.concatenate([high, mid, rest - mid], axis=0).astype(jnp.bfloat16)


def joined(y):
    rows = y.shape[0] // 3
    return y[:rows] + y[rows : 2 * rows] + y[2 * rows :]


def group_turn(pieces, out_group, group, lanes_per):
    total = None
    for a, piece in enumerate(pieces):
        shift = ((a - out_group) * lanes_per) % LANES
        moved = piece if shift == 0 else pltpu.roll(piece, shift, 1)
        total = moved if total is None else jnp.where(group == a, moved, total)
    return total


def loop(count, body):
    if count <= 8:
        for i in range(count):
            body(i)
    else:
        def step(i, carry):
            body(i)
            return carry

        lax.fori_loop(0, count, step, 0)


def summed(count, body, rows, columns):
    acc = jnp.zeros((rows, columns), jnp.float32)
    if count <= 8:
        for i in range(count):
            acc = acc + body(i)
        return acc
    return lax.fori_loop(0, count, lambda i, total: total + body(i), acc)


def aligned(start, size, unit=8):
    if not isinstance(start, int):
        start = pl.multiple_of(start, unit)
    return pl.ds(start, size)


def kernel(
    sizes,
    points,
    poses,
    angles,
    voxel_ids,
    scan_ids,
    hess_out,
    grad_out,
    cost_out,
    pts,
    pose_in,
    angle_in,
    vox_in,
    scan_in,
    pose_pad,
    sent,
    send1,
    recv1,
    pair_n,
    recv_n,
    scan_hot,
    vox_hot,
    table,
    world,
    send_a,
    recv_a,
    total_a,
    normals,
    quads,
    send_q,
    recv_q,
    send_c,
    recv_c,
    terms,
    late,
    send_h,
    recv_h,
    send_g,
    recv_g,
    lines,
    pts_sem,
    in_sem,
    sends,
    recvs,
):
    n_tm, n_map, slots, npoints, scale = sizes
    reducers = n_map // SHARE
    blocks = pts.shape[1]
    chunks = blocks // LANES
    per = LANES // slots
    own_scans = pose_in.shape[1]
    spread = LANES // own_scans
    scans = own_scans * n_map
    wide = scans // LANES
    voxels = angle_in.shape[1]
    halves = voxels // LANES
    parts = n_tm // per
    step = SHARE * parts
    arrived = n_map * step
    couples = n_map // 2 * parts
    message = step * TILE
    n_size = pair_n.shape[0] // SHARE
    a_rows = 2 * n_tm
    a_size = SHARE * halves * a_rows
    tm = lax.axis_index("tm")
    mp = lax.axis_index("map")
    rd = mp // SHARE
    part = lax.rem(mp, SHARE)
    reduces = part == SHARE - 1
    f32, bf16 = jnp.float32, jnp.bfloat16

    small = [
        pltpu.make_async_copy(src, dst, in_sem.at[i])
        for i, (src, dst) in enumerate(
            [(poses, pose_in), (angles, angle_in), (voxel_ids, vox_in), (scan_ids, scan_in)]
        )
    ]
    loads = pts_sem.shape[0]
    span = blocks // loads

    def points_copy(r):
        rows = pl.ds(r * span, span)
        return pltpu.make_async_copy(points.at[:, rows, :], pts.at[:, rows, :], pts_sem.at[r])

    for copy in small:
        copy.start()
    loop(loads, lambda r: points_copy(r).start())
    barrier = pltpu.get_barrier_semaphore()
    near = (tm, rd * SHARE + SHARE - 1)
    first_of = (tm, rd * SHARE)
    plane = [(tm, lax.rem(mp + i, n_map)) for i in range(1, n_map)]
    column = [(lax.rem(tm + i, n_tm), mp) for i in range(1, n_tm)]
    others = [lax.rem(rd + i, reducers) for i in range(1, reducers)]

    def greet(peer):
        pl.semaphore_signal(barrier, inc=1, device_id=peer, device_id_type=MESH)

    @pl.when(reduces)
    def _():
        for peer in column + plane:
            greet(peer)

    @pl.when(jnp.logical_not(reduces))
    def _():
        for other in others:
            greet((tm, other * SHARE + SHARE - 1))
        greet(near)

    def send(source, dest, peer, s):
        pltpu.make_async_remote_copy(
            src_ref=source,
            dst_ref=dest,
            send_sem=sends.at[0],
            recv_sem=recvs.at[s],
            device_id=peer,
            device_id_type=MESH,
        ).start()

    def wait_rows(rows, sem):
        ref = pts.at[0, pl.ds(0, rows), :]
        pltpu.make_async_copy(ref, ref, sem).wait()

    def every(ref, k, stride, count=arrived):
        return ref[pl.ds(k, count, stride=stride), :]

    lane = lax.broadcasted_iota(jnp.int32, (8, LANES), 1)
    group = lane // slots
    chunk_of = lax.broadcasted_iota(jnp.int32, (arrived, LANES), 0)
    turn_of = (
        lax.broadcasted_iota(jnp.int32, (arrived, LANES), 1) // slots + per * lax.rem(chunk_of, parts)
    )
    own_turn = [turn_of == t for t in range(n_tm)]
    sent[...] = jnp.zeros_like(sent)

    for copy in small:
        copy.wait()
    pose_pad[...] = jnp.zeros_like(pose_pad)
    for g in range(spread):
        pose_pad[0:6, g * own_scans : (g + 1) * own_scans] = pose_in[...]
    pose = pose_pad[...]
    cos, sin = jnp.cos(pose), jnp.sin(pose)
    cx, cy, cz = cos[0:1], cos[1:2], cos[2:3]
    sx, sy, sz = sin[0:1], sin[1:2], sin[2:3]
    pose_rows = [
        [cz * cy, cz * sy * sx - sz * cx, cz * sy * cx + sz * sx],
        [sz * cy, sz * sy * sx + cz * cx, sz * sy * cx - cz * sx],
        [-sy, cy * sx, cy * cx],
        [pose[3:4], pose[4:5], pose[5:6]],
    ]
    scan_group = lane[0:1] // own_scans
    pose_lines = []
    for q in range(3):
        line = pose_rows[0][q]
        for g in range(1, 4):
            line = jnp.where(scan_group == g, pose_rows[g][q], line)
        pose_lines.append(line)

    ids = vox_in[...]
    row_of = lax.broadcasted_iota(jnp.int32, ids.shape, 0)
    lane_of = lax.broadcasted_iota(jnp.int32, ids.shape, 1)
    owner_of = row_of * per + lane_of // slots
    local_ids = jnp.where(ids >= 0, ids - owner_of * voxels, -1).astype(f32)
    sent[pl.ds(VOX_ROW, chunks, stride=TILE), :] = local_ids
    sent[pl.ds(SCAN_ROW, chunks, stride=TILE), :] = scan_in[...].astype(f32)

    theta, phi = angle_in[0:1, :], angle_in[1:2, :]
    sin_theta = jnp.sin(theta)
    own_normal = [sin_theta * jnp.cos(phi), sin_theta * jnp.sin(phi), jnp.cos(theta)]
    n_mine = aligned(part * n_size, n_size)
    for c in range(3):
        for h in range(halves):
            k = part * n_size + c * halves + h
            pair_n[pl.ds(k, 1), :] = own_normal[c][:, h * LANES : (h + 1) * LANES]

    def raw_moments(r):
        at = aligned(r * LANES, LANES, LANES)
        xyz = [pts[i, at, :].T for i in range(3)]
        sums = [jnp.sum(x, axis=0, keepdims=True) for x in xyz]
        sums += [jnp.sum(xyz[i] * xyz[j], axis=0, keepdims=True) for i, j in PAIRS]
        for k, row in enumerate(sums):
            sent[pl.ds(r * TILE + k, 1), :] = row

    def load_step(r):
        points_copy(r).wait()
        for i in range(span // LANES):
            raw_moments(r * (span // LANES) + i)

    loop(loads, load_step)
    row_chunks = n_map // per

    def pack(peer_row):
        for g in range(per):
            peer = peer_row * per + g
            for u in range(parts):
                for half in range(2):
                    pieces = [
                        sent[
                            aligned(
                                ((u * per + a) * row_chunks + peer_row) * TILE + 8 * half, 8
                            ),
                            :,
                        ]
                        for a in range(per)
                    ]
                    at = aligned((peer * parts + u) * TILE + 8 * half, 8)
                    send1[at, :] = group_turn(pieces, g, group, slots)
            for q in range(3):
                send1[pl.ds(peer * parts * TILE + POSE_ROW + q, 1), :] = pose_lines[q]

    loop(row_chunks, pack)

    from_plane = n_map - 1 + n_tm - 1
    pl.semaphore_wait(barrier, jnp.where(reduces, from_plane, reducers))
    mine = aligned(mp * message, message)

    def message_of(other):
        return send1.at[aligned(other * message, message), :]

    @pl.when(jnp.logical_not(reduces))
    def _():
        send(pair_n.at[n_mine, :], pair_n.at[n_mine, :], near, 6)

    for other in others:
        send(message_of(other), recv1.at[mine, :], (tm, other * SHARE + SHARE - 1), 0)

    @pl.when(jnp.logical_not(reduces))
    def _():
        send(message_of(rd), recv1.at[mine, :], near, 0)

    eight = aligned(rd * 8, 8)

    def reduce_part():
        wait_rows(n_size, recvs.at[6])
        n_column = aligned(tm * SHARE * n_size, SHARE * n_size)
        for peer in column:
            send(pair_n, recv_n.at[n_column, :], peer, 1)
        recv1[mine, :] = send1[aligned(rd * message, message), :]
        recv_n[n_column, :] = pair_n[...]
        for t in range(n_tm):
            world[pl.ds(3 * n_tm + t, arrived, stride=4 * n_tm), :] = jnp.where(
                own_turn[t], 1.0, 0.0
            )
        quads[...] = jnp.zeros_like(quads)
        late[...] = jnp.zeros_like(late)
        wait_rows((n_map - 1) * message, recvs.at[0])

        def chunk(k, q, side):
            i, u = (q // parts, q % parts) if isinstance(q, int) else (q // parts, lax.rem(q, parts))
            return ((2 * i + side) * SHARE + k) * parts + u

        def couple_row(k, q, row):
            return jnp.concatenate(
                [recv1[pl.ds(chunk(k, q, side) * TILE + row, 1), :] for side in range(2)], axis=1
            )

        def couple_tile(ref, k, q, rows):
            return jnp.concatenate(
                [ref[aligned(chunk(k, q, side) * rows, rows), :] for side in range(2)], axis=1
            )

        def spread_out(ref, k, q, rows, value):
            for side in range(2):
                ref[aligned(chunk(k, q, side) * rows, rows), :] = value[
                    :, side * LANES : (side + 1) * LANES
                ]

        def each_couple(body):
            for k in range(SHARE):
                loop(couples, functools.partial(body, k))

        scan_iota = lax.broadcasted_iota(jnp.int32, (scans, 2 * LANES), 0).astype(f32)
        vox_iota = lax.broadcasted_iota(jnp.int32, (voxels, 2 * LANES), 0).astype(f32)

        def mark(k, q):
            scan_hot[k * couples + q] = jnp.where(
                couple_row(k, q, SCAN_ROW) == scan_iota, 1.0, 0.0
            ).astype(bf16)
            vox_hot[k * couples + q] = jnp.where(
                couple_row(k, q, VOX_ROW) == vox_iota, 1.0, 0.0
            ).astype(bf16)

        top = lax.broadcasted_iota(jnp.int32, (8, LANES), 0) < 4
        own_group = lane // own_scans
        columns = []
        for h in range(wide):
            at = [(h * spread + a) * message + 8 for a in range(spread)]
            tiles = [recv1[row : row + 8, :] for row in at]
            turned = [group_turn(tiles, g, own_group, own_scans) for g in range(4)]
            low = jnp.where(top, pltpu.roll(turned[1], 4, 0), turned[0])
            high = jnp.where(top, pltpu.roll(turned[3], 4, 0), turned[2])
            columns.append(jnp.concatenate([low, high], axis=0))
        pose_table = split(jnp.concatenate(columns, axis=1))
        table_row = {}
        for q in range(3):
            table_row[(1, q)], table_row[(0, q)] = q, 4 + q
            table_row[(3, q)], table_row[(2, q)] = 8 + q, 12 + q

        def look_up(k, q):
            mark(k, q)
            found = jnp.dot(pose_table, scan_hot[k * couples + q], preferred_element_type=f32)
            spread_out(table, k, q, TILE, joined(found))

        each_couple(look_up)
        rot = [[every(table, table_row[(i, j)], TILE) for j in range(3)] for i in range(3)]
        shift = [every(table, table_row[(3, j)], TILE) for j in range(3)]
        first = [every(recv1, k, TILE) for k in range(3)]
        turned_first = [sum(rot[i][j] * first[j] for j in range(3)) for i in range(3)]
        m1 = [turned_first[i] + npoints * shift[i] for i in range(3)]
        for c in range(3):
            for t in range(n_tm):
                world[pl.ds(c * n_tm + t, arrived, stride=4 * n_tm), :] = jnp.where(
                    own_turn[t], m1[c], 0.0
                )

        def voxel_sums(ref, rows, k):
            def add(q):
                return lax.dot_general(
                    split(couple_tile(ref, k, q, rows)),
                    vox_hot[k * couples + q],
                    CONTRACT_LAST,
                    preferred_element_type=f32,
                )

            return joined(summed(couples, add, 3 * rows, voxels))

        sums = [voxel_sums(world, 4 * n_tm, k) for k in range(SHARE)]
        wait_rows((n_tm - 1) * SHARE * n_size, recvs.at[1])
        normal = [
            [
                jnp.concatenate(
                    [
                        every(recv_n, k * n_size + c * halves + h, SHARE * n_size, n_tm)
                        for h in range(halves)
                    ],
                    axis=1,
                )
                for c in range(3)
            ]
            for k in range(SHARE)
        ]
        for k in range(SHARE):
            along = sum(normal[k][c] * sums[k][c * n_tm : (c + 1) * n_tm] for c in range(3))
            count = sums[k][3 * n_tm : 4 * n_tm]
            for h in range(halves):
                at = slice(h * LANES, (h + 1) * LANES)
                base = (k * halves + h) * a_rows
                send_a[base : base + n_tm, :] = along[:, at]
                send_a[base + n_tm : base + a_rows, :] = count[:, at]

        a_mine = aligned(tm * a_size, a_size)
        for peer in column:
            send(send_a, recv_a.at[a_mine, :], peer, 2)
        recv_a[a_mine, :] = send_a[...]

        normal_table = [
            split(jnp.concatenate(normal[k] + [jnp.zeros_like(normal[k][0])], axis=0))
            for k in range(SHARE)
        ]

        def find_normals(k, q):
            found = jnp.dot(normal_table[k], vox_hot[k * couples + q], preferred_element_type=f32)
            spread_out(normals, k, q, 4 * n_tm, joined(found))

        each_couple(find_normals)
        n = []
        for c in range(3):
            value = every(normals, c * n_tm, 4 * n_tm)
            for t in range(1, n_tm):
                value = jnp.where(own_turn[t], every(normals, c * n_tm + t, 4 * n_tm), value)
            n.append(value)
        second = [every(recv1, 3 + k, TILE) for k in range(6)]
        half_turned = [
            [sum(rot[i][k] * second[PAIR_ROW[(k, j)]] for k in range(3)) for j in range(3)]
            for i in range(3)
        ]
        m2 = [
            sum(half_turned[i][k] * rot[j][k] for k in range(3))
            + turned_first[i] * shift[j]
            + shift[i] * m1[j]
            for i, j in PAIRS
        ]
        quad = sum(n[i] ** 2 * m2[i] for i in range(3)) + 2.0 * sum(
            n[PAIRS[k][0]] * n[PAIRS[k][1]] * m2[k] for k in range(3, 6)
        )
        for t in range(n_tm):
            quads[pl.ds(t, arrived, stride=8), :] = jnp.where(own_turn[t], quad, 0.0)
        for k in range(SHARE):
            quad_sums = voxel_sums(quads, 8, k)
            for t in range(n_tm):
                for h in range(halves):
                    send_q[t, k * halves + h : k * halves + h + 1, :] = quad_sums[
                        t : t + 1, h * LANES : (h + 1) * LANES
                    ]
        for peer in column:
            send(send_q.at[peer[0]], recv_q.at[tm], peer, 3)
        recv_q[tm] = send_q[tm]

        def skew(v):
            return [
                n[2] * v[1] - n[1] * v[2],
                n[0] * v[2] - n[2] * v[0],
                n[1] * v[0] - n[0] * v[1],
            ]

        full = [[m2[PAIR_ROW[(i, j)]] for j in range(3)] for i in range(3)]
        skewed = [skew([full[k][j] for k in range(3)]) for j in range(3)]
        left = [[skewed[j][i] for j in range(3)] for i in range(3)]
        corner_block = [skew(left[i]) for i in range(3)]
        skew_first = skew(m1)
        found = {}
        for i in range(3):
            for j in range(3):
                if j >= i:
                    found[("h", i, j)] = corner_block[i][j]
                    found[("h", 3 + i, 3 + j)] = npoints * n[i] * n[j]
                found[("h", i, 3 + j)] = skew_first[i] * n[j]
        rest = n[0] * m1[0] + n[1] * m1[1] + n[2] * m1[2]
        for i in range(3):
            found[("g", i)] = sum(left[i][j] * n[j] for j in range(3))
            found[("g", 3 + i)] = n[i] * rest
            late[pl.ds(i, arrived, stride=8), :] = skew_first[i]
            late[pl.ds(3 + i, arrived, stride=8), :] = npoints * n[i]
        for name, value in found.items():
            terms[pl.ds(ROWS.index(name), arrived, stride=32), :] = value
        for k in range(len(found), 32):
            terms[pl.ds(k, arrived, stride=32), :] = jnp.zeros_like(rest)

        def scan_sums(k, tile, rows):
            def add(q):
                return lax.dot_general(
                    split(tile(k, q)),
                    scan_hot[k * couples + q],
                    CONTRACT_LAST,
                    preferred_element_type=f32,
                )

            return summed(couples, add, 3 * rows, scans)

        per_scan = scale * joined(
            sum(scan_sums(k, lambda k, q: couple_tile(terms, k, q, 32), 32) for k in range(SHARE))
        )
        for h in range(wide):
            pieces = [per_scan[8 * c : 8 * c + 8, h * LANES : (h + 1) * LANES] for c in range(4)]
            for b in range(spread):
                at = (h * spread + b) * 8
                send_h[at : at + 8, :] = group_turn(pieces, b, own_group, own_scans)
        for peer in plane:
            send(send_h.at[aligned(peer[1] * 8, 8), :], recv_h.at[eight, :], peer, 4)
        recv_h[eight, :] = send_h[aligned(mp * 8, 8), :]

        wait_rows((n_tm - 1) * a_size, recvs.at[2])
        offset_table = []
        for k in range(SHARE):
            offsets = []
            for h in range(halves):
                base = (k * halves + h) * a_rows
                total = recv_a[base : base + a_rows, :]
                for t in range(1, n_tm):
                    total = total + recv_a[t * a_size + base : t * a_size + base + a_rows, :]
                floor = jnp.maximum(total[n_tm:] * npoints, 1.0)
                offset = total[:n_tm] / floor
                total_a[base : base + n_tm, :] = offset
                total_a[base + n_tm : base + a_rows, :] = floor
                offsets.append(offset)
            offset = jnp.concatenate(offsets, axis=1)
            if n_tm % 8:
                offset = jnp.concatenate(
                    [offset, jnp.zeros((8 - n_tm % 8, voxels), f32)], axis=0
                )
            offset_table.append(split(offset))
        d_rows = offset.shape[0]
        turn_row = lax.broadcasted_iota(jnp.int32, (d_rows, 2 * LANES), 0)
        turn_lane = lax.rem(lax.broadcasted_iota(jnp.int32, turn_row.shape, 1), LANES) // slots

        def late_tile(k, q):
            value = joined(
                jnp.dot(offset_table[k], vox_hot[k * couples + q], preferred_element_type=f32)
            )
            turn = turn_lane
            if parts > 1:
                turn = turn + per * lax.rem(q, parts)
            d = jnp.sum(jnp.where(turn_row == turn, value, 0.0), axis=0, keepdims=True)
            return couple_tile(late, k, q, 8) * d

        moved = scale * joined(sum(scan_sums(k, late_tile, 8) for k in range(SHARE)))
        for h in range(wide):
            send_g[h * 8 : h * 8 + 8, :] = moved[:, h * LANES : (h + 1) * LANES]
        for peer in plane:
            source = send_g.at[aligned(peer[1] // spread * 8, 8), :]
            send(source, recv_g.at[eight, :], peer, 5)
        recv_g[eight, :] = send_g[aligned(mp // spread * 8, 8), :]

        pltpu.make_async_copy(
            recv_q.at[pl.ds(0, n_tm - 1)], recv_q.at[pl.ds(0, n_tm - 1)], recvs.at[3]
        ).wait()
        quad_total = recv_q[0]
        for t in range(1, n_tm):
            quad_total = quad_total + recv_q[t]
        own_offset = total_a[pl.ds(tm, SHARE * halves, stride=a_rows), :]
        own_floor = total_a[pl.ds(n_tm + tm, SHARE * halves, stride=a_rows), :]
        cost = quad_total / own_floor - own_offset**2
        send_c[...] = cost[0:halves]
        send(send_c, recv_c, first_of, 7)
        recv_c[...] = cost[halves:]

    pl.when(reduces)(reduce_part)


    def wait_plane(s):
        @pl.when(reduces)
        def _():
            wait_rows((reducers - 1) * 8, recvs.at[s])

        @pl.when(jnp.logical_not(reduces))
        def _():
            wait_rows(reducers * 8, recvs.at[s])

    lines[...] = jnp.zeros_like(lines)
    wait_plane(4)
    total = recv_h[0:8, :]
    for m in range(1, reducers):
        total = total + recv_h[m * 8 : m * 8 + 8, :]
    lined = [total] + [pltpu.roll(total, LANES - own_scans * c, 1) for c in range(1, 4)]

    def row_at(name):
        k = ROWS.index(name)
        return lined[k // 8][k % 8 : k % 8 + 1]

    for i in range(6):
        for j in range(6):
            lines[6 * i + j : 6 * i + j + 1, :] = row_at(("h", min(i, j), max(i, j)))
    hess_out[...] = lines[...].T[0:own_scans, 0:36]
    gradient = jnp.concatenate([row_at(("g", i)) for i in range(6)], axis=0)

    @pl.when(jnp.logical_not(reduces))
    def _():
        pltpu.make_async_copy(recv_c, recv_c, recvs.at[7]).wait()

    for h in range(halves):
        cost_out[:, h * LANES : (h + 1) * LANES] = recv_c[h : h + 1, :]

    wait_plane(5)
    change = recv_g[0:8, :]
    for m in range(1, reducers):
        change = change + recv_g[m * 8 : m * 8 + 8, :]
    change = pltpu.roll(change, LANES - own_scans * lax.rem(mp, spread), 1)
    grad_out[...] = (gradient - change[0:6])[:, 0:own_scans]

    @pl.when(reduces)
    def _():
        rows = (reducers - 1) * message + (n_map - 1) * 16 + halves
        rows += (n_tm - 1) * (SHARE * n_size + a_size + SHARE * halves)
        wait_rows(rows, sends.at[0])

    @pl.when(jnp.logical_not(reduces))
    def _():
        wait_rows(reducers * message + n_size, sends.at[0])


def finish(hess_in, grad_in, cost_in, hess_out, grad_out, cost_out, sems):
    copies = [
        pltpu.make_async_copy(src, dst, sems.at[i])
        for i, (src, dst) in enumerate(
            [(hess_in, hess_out), (grad_in, grad_out), (cost_in, cost_out)]
        )
    ]
    for copy in copies:
        copy.start()
    for copy in copies:
        copy.wait()


def local(points, poses, normal_angles, voxel_ids, scan_ids):
    blocks, npoints = points.shape[1:]
    n_tm, n_map = lax.axis_size("tm"), lax.axis_size("map")
    devices = n_tm * n_map
    slots = blocks // devices
    chunks = blocks // LANES
    vox_count = normal_angles.shape[1]
    own_scans = poses.shape[1]
    assert npoints == LANES and slots * 4 == LANES and own_scans * 4 == LANES
    assert n_map % 4 == 0 and n_map % SHARE == 0 and n_tm % 4 == 0 and vox_count % LANES == 0
    scale = own_scans * devices / (blocks * devices * npoints)
    f32, bf16 = jnp.float32, jnp.bfloat16
    scans = own_scans * n_map
    halves = vox_count // LANES
    sent_rows = n_map * n_tm // 4 * TILE
    arrived = SHARE * n_map * n_tm // 4
    n_rows = -(-3 * halves // 8) * 8
    a_rows = SHARE * 2 * n_tm * halves
    reducers = n_map // SHARE
    hbm = pl.BlockSpec(memory_space=pl.ANY)
    vmem = pl.BlockSpec(memory_space=pltpu.VMEM)
    shapes = [(own_scans, 36), (6, own_scans), (1, vox_count)]
    results = pl.pallas_call(
        functools.partial(kernel, (n_tm, n_map, slots, float(npoints), scale)),
        out_shape=tuple(pltpu.VMEM(shape, f32) for shape in shapes),
        in_specs=[hbm] * 5,
        out_specs=(vmem,) * 3,
        scratch_shapes=[
            pltpu.VMEM(points.shape, f32),
            pltpu.VMEM(poses.shape, f32),
            pltpu.VMEM(normal_angles.shape, f32),
            pltpu.VMEM((chunks, LANES), jnp.int32),
            pltpu.VMEM((chunks, LANES), jnp.int32),
            pltpu.VMEM((8, LANES), f32),
            pltpu.VMEM((chunks * TILE, LANES), f32),
            pltpu.VMEM((sent_rows, LANES), f32),
            pltpu.VMEM((arrived * TILE, LANES), f32),
            pltpu.VMEM((SHARE * n_rows, LANES), f32),
            pltpu.VMEM((n_tm * SHARE * n_rows, LANES), f32),
            pltpu.VMEM((arrived // 2, scans, 2 * LANES), bf16),
            pltpu.VMEM((arrived // 2, vox_count, 2 * LANES), bf16),
            pltpu.VMEM((arrived * TILE, LANES), f32),
            pltpu.VMEM((arrived * 4 * n_tm, LANES), f32),
            pltpu.VMEM((a_rows, LANES), f32),
            pltpu.VMEM((n_tm * a_rows, LANES), f32),
            pltpu.VMEM((a_rows, LANES), f32),
            pltpu.VMEM((arrived * 4 * n_tm, LANES), f32),
            pltpu.VMEM((arrived * 8, LANES), f32),
            pltpu.VMEM((n_tm, SHARE * halves, LANES), f32),
            pltpu.VMEM((n_tm, SHARE * halves, LANES), f32),
            pltpu.VMEM((halves, LANES), f32),
            pltpu.VMEM((halves, LANES), f32),
            pltpu.VMEM((arrived * 32, LANES), f32),
            pltpu.VMEM((arrived * 8, LANES), f32),
            pltpu.VMEM((n_map * 8, LANES), f32),
            pltpu.VMEM((reducers * 8, LANES), f32),
            pltpu.VMEM((scans // LANES * 8, LANES), f32),
            pltpu.VMEM((reducers * 8, LANES), f32),
            pltpu.VMEM((LANES, LANES), f32),
            pltpu.SemaphoreType.DMA((4,)),
            pltpu.SemaphoreType.DMA((4,)),
            pltpu.SemaphoreType.DMA((1,)),
            pltpu.SemaphoreType.DMA((8,)),
        ],
        compiler_params=pltpu.CompilerParams(collective_id=0, has_side_effects=True),
    )(
        points,
        poses,
        normal_angles,
        voxel_ids.reshape(chunks, LANES),
        scan_ids.reshape(chunks, LANES),
    )
    hess, grad, cost = pl.pallas_call(
        finish,
        out_shape=tuple(jax.ShapeDtypeStruct(shape, f32) for shape in shapes),
        in_specs=[vmem] * 3,
        out_specs=(hbm,) * 3,
        scratch_shapes=[pltpu.SemaphoreType.DMA((3,))],
    )(*[pltpu.with_memory_space_constraint(x, pltpu.VMEM) for x in results])
    return hess.T, grad, cost.reshape(vox_count)


def solution(mesh):
    return jax.shard_map(
        local,
        mesh=mesh,
        in_specs=(
            P(None, ("tm", "map"), None),
            P(None, ("tm", "map")),
            P(None, ("tm", "map")),
            P(("tm", "map")),
            P(("tm", "map")),
        ),
        out_specs=(P(None, ("tm", "map")), P(None, ("tm", "map")), P(("tm", "map"))),
        check_vma=False,
    )
```

time: 18.5 us -> 17.4 us (0.941)
  Pallas kernels: 17.7 us -> 16.6 us
    pallas_call x1, Pallas kernels: 17.1 us -> 16 us  [local(): pl.pallas_call(functools.partial(kernel, (n_tm, n_map, slots, float(npoin...]
where the time goes in v3:
time: 17.4 us; the launch traced here: 17.3 us
  Pallas kernels  16.6 us (95%)
  between operations  0.64 us (4%)
    pallas_call x1, Pallas kernels, local(): pl.pallas_call(functools.partial(kernel, (n_tm, n_map, slots, float(npoin...  16 us
    pallas_call x1, Pallas kernels, local(): pl.pallas_call(finish, out_shape=tuple((jax.ShapeDtypeStruct(shape, f32)...  0.64 us

profile of v3, /device:TPU:0, one launch (start us, length us, event | category | flops | bytes accessed | tf_op | source)
XLA Modules:
  0.0 17.3 jit_solution(11211496569518925152)
XLA Ops:
  0.6 16.0 %shard_map.76 = (f32[32,36]{1,0:T(8,128)S(1)}, f32[6,32]{1,0:T(8,128)S(1)}, f32[1,256]{1,0:T(1,128)S(1)}) custom-call(f32[3,1024,128]{2,1,0:T(8,128)} %points.1, f32[6,32]{1,0:T(8,128)} %poses.1, f32[2,256]{1,0:T(2,128)} %angles.1, s32[8,128]{1,0:T(8,128)} %bitcast.4, s32[8,128]{1,0:T(8,128)} %bitcast.5), custom_call_target="tpu_custom_call" | custom-call | tf_op jit(solution)/shard_map/pallas_call | solution.py:669
  16.6 0.6 %shard_map.77 = (f32[32,36]{1,0:T(8,128)}, f32[6,32]{1,0:T(8,128)}, f32[1,256]{1,0:T(1,128)}) custom-call(f32[32,36]{1,0:T(8,128)S(1)} %get-tuple-element.9.hess_in, f32[6,32]{1,0:T(8,128)S(1)} %get-tuple-element.10.grad_in, f32[1,256]{1,0:T(1,128)S(1)} %get-tuple-element.11.cost_in), custom_call_target="tpu_custom_call" | custom-call | tf_op jit(solution)/shard_map/pallas_call | solution.py:719

commit v4 on v3

--- a/solution.py
+++ b/solution.py
@@ -94,12 +94,10 @@
     recv_n,
     scan_hot,
     vox_hot,
-    table,
     world,
     send_a,
     recv_a,
     total_a,
-    normals,
     quads,
     send_q,
     recv_q,
@@ -173,6 +171,11 @@
     def _():
         for peer in column + plane:
             greet(peer)
+        for peer in column:
+
+            @pl.when(peer[0] > tm)
+            def _(peer=peer):
+                greet((peer[0], rd * SHARE))
 
     @pl.when(jnp.logical_not(reduces))
     def _():
@@ -284,14 +287,23 @@
     loop(row_chunks, pack)
 
     from_plane = n_map - 1 + n_tm - 1
-    pl.semaphore_wait(barrier, jnp.where(reduces, from_plane, reducers))
+    pl.semaphore_wait(barrier, jnp.where(reduces, from_plane, reducers + tm))
     mine = aligned(mp * message, message)
 
     def message_of(other):
         return send1.at[aligned(other * message, message), :]
 
+    def normals_to(t, k):
+        return recv_n.at[aligned((t * SHARE + k) * n_size, n_size), :]
+
     @pl.when(jnp.logical_not(reduces))
     def _():
+        for peer in column:
+
+            @pl.when(peer[0] < tm)
+            def _(peer=peer):
+                send(pair_n.at[n_mine, :], normals_to(tm, 0), (peer[0], near[1]), 1)
+
         send(pair_n.at[n_mine, :], pair_n.at[n_mine, :], near, 6)
 
     for other in others:
@@ -304,10 +316,16 @@
     eight = aligned(rd * 8, 8)
 
     def reduce_part():
+        for peer in column:
+            send(pair_n.at[pl.ds(n_size, n_size), :], normals_to(tm, 1), peer, 1)
         wait_rows(n_size, recvs.at[6])
+        for peer in column:
+
+            @pl.when(peer[0] > tm)
+            def _(peer=peer):
+                send(pair_n.at[pl.ds(0, n_size), :], normals_to(tm, 0), peer, 1)
+
         n_column = aligned(tm * SHARE * n_size, SHARE * n_size)
-        for peer in column:
-            send(pair_n, recv_n.at[n_column, :], peer, 1)
         recv1[mine, :] = send1[aligned(rd * message, message), :]
         recv_n[n_column, :] = pair_n[...]
         for t in range(n_tm):
@@ -332,12 +350,6 @@
                 [ref[aligned(chunk(k, q, side) * rows, rows), :] for side in range(2)], axis=1
             )
 
-        def spread_out(ref, k, q, rows, value):
-            for side in range(2):
-                ref[aligned(chunk(k, q, side) * rows, rows), :] = value[
-                    :, side * LANES : (side + 1) * LANES
-                ]
-
         def each_couple(body):
             for k in range(SHARE):
                 loop(couples, functools.partial(body, k))
@@ -345,10 +357,12 @@
         scan_iota = lax.broadcasted_iota(jnp.int32, (scans, 2 * LANES), 0).astype(f32)
         vox_iota = lax.broadcasted_iota(jnp.int32, (voxels, 2 * LANES), 0).astype(f32)
 
-        def mark(k, q):
+        def mark_scans(k, q):
             scan_hot[k * couples + q] = jnp.where(
                 couple_row(k, q, SCAN_ROW) == scan_iota, 1.0, 0.0
             ).astype(bf16)
+
+        def mark_voxels(k, q):
             vox_hot[k * couples + q] = jnp.where(
                 couple_row(k, q, VOX_ROW) == vox_iota, 1.0, 0.0
             ).astype(bf16)
@@ -363,20 +377,31 @@
             low = jnp.where(top, pltpu.roll(turned[1], 4, 0), turned[0])
             high = jnp.where(top, pltpu.roll(turned[3], 4, 0), turned[2])
             columns.append(jnp.concatenate([low, high], axis=0))
-        pose_table = split(jnp.concatenate(columns, axis=1))
         table_row = {}
         for q in range(3):
             table_row[(1, q)], table_row[(0, q)] = q, 4 + q
             table_row[(3, q)], table_row[(2, q)] = 8 + q, 12 + q
 
-        def look_up(k, q):
-            mark(k, q)
-            found = jnp.dot(pose_table, scan_hot[k * couples + q], preferred_element_type=f32)
-            spread_out(table, k, q, TILE, joined(found))
-
-        each_couple(look_up)
-        rot = [[every(table, table_row[(i, j)], TILE) for j in range(3)] for i in range(3)]
-        shift = [every(table, table_row[(3, j)], TILE) for j in range(3)]
+        def whole_row(row, count):
+            return jnp.broadcast_to(row, (count, LANES))
+
+        def gather(tables, high, low):
+            value = jnp.take_along_axis(tables[0], low, axis=1, mode="promise_in_bounds")
+            for h in range(1, len(tables)):
+                other = jnp.take_along_axis(tables[h], low, axis=1, mode="promise_in_bounds")
+                value = jnp.where(high == h, other, value)
+            return value
+
+        scan_of = every(recv1, SCAN_ROW, TILE).astype(jnp.int32)
+        scan_low, scan_high = jnp.bitwise_and(scan_of, LANES - 1), scan_of // LANES
+
+        def pose_of(i, j):
+            row = table_row[(i, j)]
+            rows = [whole_row(tile[row : row + 1], arrived) for tile in columns]
+            return gather(rows, scan_high, scan_low)
+
+        rot = [[pose_of(i, j) for j in range(3)] for i in range(3)]
+        shift = [pose_of(3, j) for j in range(3)]
         first = [every(recv1, k, TILE) for k in range(3)]
         turned_first = [sum(rot[i][j] * first[j] for j in range(3)) for i in range(3)]
         m1 = [turned_first[i] + npoints * shift[i] for i in range(3)]
@@ -385,6 +410,8 @@
                 world[pl.ds(c * n_tm + t, arrived, stride=4 * n_tm), :] = jnp.where(
                     own_turn[t], m1[c], 0.0
                 )
+
+        each_couple(mark_voxels)
 
         def voxel_sums(ref, rows, k):
             def add(q):
@@ -426,22 +453,32 @@
             send(send_a, recv_a.at[a_mine, :], peer, 2)
         recv_a[a_mine, :] = send_a[...]
 
-        normal_table = [
-            split(jnp.concatenate(normal[k] + [jnp.zeros_like(normal[k][0])], axis=0))
-            for k in range(SHARE)
-        ]
-
-        def find_normals(k, q):
-            found = jnp.dot(normal_table[k], vox_hot[k * couples + q], preferred_element_type=f32)
-            spread_out(normals, k, q, 4 * n_tm, joined(found))
-
-        each_couple(find_normals)
+        each_couple(mark_scans)
+        vox_of = every(recv1, VOX_ROW, TILE).astype(jnp.int32)
+        live = vox_of >= 0
+        vox_low = jnp.bitwise_and(vox_of, LANES - 1)
+        vox_high = jnp.where(live, vox_of, 0) // LANES
+        part_of = lax.rem(lax.broadcasted_iota(jnp.int32, (step, LANES), 0) // parts, SHARE)
+
+        def by_voxel(rows):
+            value = None
+            for t in range(n_tm):
+                tables = []
+                for h in range(halves):
+                    tab = whole_row(rows(0, t, h), step)
+                    for k in range(1, SHARE):
+                        tab = jnp.where(part_of == k, whole_row(rows(k, t, h), step), tab)
+                    tables.append(jnp.concatenate([tab] * n_map, axis=0))
+                found = gather(tables, vox_high, vox_low)
+                value = found if t == 0 else jnp.where(own_turn[t], found, value)
+            return value
+
         n = []
         for c in range(3):
-            value = every(normals, c * n_tm, 4 * n_tm)
-            for t in range(1, n_tm):
-                value = jnp.where(own_turn[t], every(normals, c * n_tm + t, 4 * n_tm), value)
-            n.append(value)
+            value = by_voxel(
+                lambda k, t, h: normal[k][c][t : t + 1, h * LANES : (h + 1) * LANES]
+            )
+            n.append(jnp.where(live, value, 0.0))
         second = [every(recv1, 3 + k, TILE) for k in range(6)]
         half_turned = [
             [sum(rot[i][k] * second[PAIR_ROW[(k, j)]] for k in range(3)) for j in range(3)]
@@ -492,8 +529,7 @@
         for i in range(3):
             found[("g", i)] = sum(left[i][j] * n[j] for j in range(3))
             found[("g", 3 + i)] = n[i] * rest
-            late[pl.ds(i, arrived, stride=8), :] = skew_first[i]
-            late[pl.ds(3 + i, arrived, stride=8), :] = npoints * n[i]
+        shares = skew_first + [npoints * n[i] for i in range(3)]
         for name, value in found.items():
             terms[pl.ds(ROWS.index(name), arrived, stride=32), :] = value
         for k in range(len(found), 32):
@@ -523,7 +559,7 @@
         recv_h[eight, :] = send_h[aligned(mp * 8, 8), :]
 
         wait_rows((n_tm - 1) * a_size, recvs.at[2])
-        offset_table = []
+        offset_rows = []
         for k in range(SHARE):
             offsets = []
             for h in range(halves):
@@ -536,27 +572,13 @@
                 total_a[base : base + n_tm, :] = offset
                 total_a[base + n_tm : base + a_rows, :] = floor
                 offsets.append(offset)
-            offset = jnp.concatenate(offsets, axis=1)
-            if n_tm % 8:
-                offset = jnp.concatenate(
-                    [offset, jnp.zeros((8 - n_tm % 8, voxels), f32)], axis=0
-                )
-            offset_table.append(split(offset))
-        d_rows = offset.shape[0]
-        turn_row = lax.broadcasted_iota(jnp.int32, (d_rows, 2 * LANES), 0)
-        turn_lane = lax.rem(lax.broadcasted_iota(jnp.int32, turn_row.shape, 1), LANES) // slots
-
-        def late_tile(k, q):
-            value = joined(
-                jnp.dot(offset_table[k], vox_hot[k * couples + q], preferred_element_type=f32)
-            )
-            turn = turn_lane
-            if parts > 1:
-                turn = turn + per * lax.rem(q, parts)
-            d = jnp.sum(jnp.where(turn_row == turn, value, 0.0), axis=0, keepdims=True)
-            return couple_tile(late, k, q, 8) * d
-
-        moved = scale * joined(sum(scan_sums(k, late_tile, 8) for k in range(SHARE)))
+            offset_rows.append(offsets)
+        offset_of = by_voxel(lambda k, t, h: offset_rows[k][h][t : t + 1])
+        for i in range(6):
+            late[pl.ds(i, arrived, stride=8), :] = shares[i] * offset_of
+        moved = scale * joined(
+            sum(scan_sums(k, lambda k, q: couple_tile(late, k, q, 8), 8) for k in range(SHARE))
+        )
         for h in range(wide):
             send_g[h * 8 : h * 8 + 8, :] = moved[:, h * LANES : (h + 1) * LANES]
         for peer in plane:
@@ -620,15 +642,17 @@
     change = pltpu.roll(change, LANES - own_scans * lax.rem(mp, spread), 1)
     grad_out[...] = (gradient - change[0:6])[:, 0:own_scans]
 
-    @pl.when(reduces)
-    def _():
-        rows = (reducers - 1) * message + (n_map - 1) * 16 + halves
-        rows += (n_tm - 1) * (SHARE * n_size + a_size + SHARE * halves)
-        wait_rows(rows, sends.at[0])
-
-    @pl.when(jnp.logical_not(reduces))
-    def _():
-        wait_rows(reducers * message + n_size, sends.at[0])
+    for t in range(n_tm):
+
+        @pl.when(jnp.logical_and(reduces, tm == t))
+        def _(t=t):
+            rows = (reducers - 1) * message + (n_map - 1) * 16 + halves
+            rows += (n_tm - 1) * (n_size + a_size + SHARE * halves) + (n_tm - 1 - t) * n_size
+            wait_rows(rows, sends.at[0])
+
+        @pl.when(jnp.logical_and(jnp.logical_not(reduces), tm == t))
+        def _(t=t):
+            wait_rows(reducers * message + (t + 1) * n_size, sends.at[0])
 
 
 def finish(hess_in, grad_in, cost_in, hess_out, grad_out, cost_out, sems):
@@ -685,12 +709,10 @@
             pltpu.VMEM((n_tm * SHARE * n_rows, LANES), f32),
             pltpu.VMEM((arrived // 2, scans, 2 * LANES), bf16),
             pltpu.VMEM((arrived // 2, vox_count, 2 * LANES), bf16),
-            pltpu.VMEM((arrived * TILE, LANES), f32),
             pltpu.VMEM((arrived * 4 * n_tm, LANES), f32),
             pltpu.VMEM((a_rows, LANES), f32),
             pltpu.VMEM((n_tm * a_rows, LANES), f32),
             pltpu.VMEM((a_rows, LANES), f32),
-            pltpu.VMEM((arrived * 4 * n_tm, LANES), f32),
             pltpu.VMEM((arrived * 8, LANES), f32),
             pltpu.VMEM((n_tm, SHARE * halves, LANES), f32),
             pltpu.VMEM((n_tm, SHARE * halves, LANES), f32),

time: 17.4 us -> 16.7 us (0.960)
  Pallas kernels: 16.6 us -> 15.9 us
    pallas_call x1, Pallas kernels: 16 us -> 15.3 us  [local(): pl.pallas_call(functools.partial(kernel, (n_tm, n_map, slots, float(npoin...]
where the time goes in v4:
time: 16.7 us; the launch traced here: 16.6 us
  Pallas kernels  15.9 us (95%)
  between operations  0.64 us (4%)
    pallas_call x1, Pallas kernels, local(): pl.pallas_call(functools.partial(kernel, (n_tm, n_map, slots, float(npoin...  15.3 us
    pallas_call x1, Pallas kernels, local(): pl.pallas_call(finish, out_shape=tuple((jax.ShapeDtypeStruct(shape, f32)...  0.64 us

profile of v4, /device:TPU:0, one launch (start us, length us, event | category | flops | bytes accessed | tf_op | source)
XLA Modules:
  0.0 16.6 jit_solution(8731757055261217350)
XLA Ops:
  0.6 15.3 %shard_map.76 = (f32[32,36]{1,0:T(8,128)S(1)}, f32[6,32]{1,0:T(8,128)S(1)}, f32[1,256]{1,0:T(1,128)S(1)}) custom-call(f32[3,1024,128]{2,1,0:T(8,128)} %points.1, f32[6,32]{1,0:T(8,128)} %poses.1, f32[2,256]{1,0:T(2,128)} %angles.1, s32[8,128]{1,0:T(8,128)} %bitcast.4, s32[8,128]{1,0:T(8,128)} %bitcast.5), custom_call_target="tpu_custom_call" | custom-call | tf_op jit(solution)/shard_map/pallas_call | solution.py:693
  15.9 0.6 %shard_map.77 = (f32[32,36]{1,0:T(8,128)}, f32[6,32]{1,0:T(8,128)}, f32[1,256]{1,0:T(1,128)}) custom-call(f32[32,36]{1,0:T(8,128)S(1)} %get-tuple-element.9.hess_in, f32[6,32]{1,0:T(8,128)S(1)} %get-tuple-element.10.grad_in, f32[1,256]{1,0:T(1,128)S(1)} %get-tuple-element.11.cost_in), custom_call_target="tpu_custom_call" | custom-call | tf_op jit(solution)/shard_map/pallas_call | solution.py:741

commit v5 on v4

--- a/solution.py
+++ b/solution.py
@@ -17,8 +17,8 @@
 
 ROWS = [("h", i, j) for i in range(6) for j in range(i, 6)] + [("g", i) for i in range(6)]
 
-TILE = 16
-VOX_ROW, SCAN_ROW, POSE_ROW = 9, 10, 12
+MARKS, FIRSTS = 0, 8
+VOX_ROW, SCAN_ROW, LAST_ROW, POSE_ROW = 0, 1, 2, 3
 SHARE = 2
 CONTRACT_LAST = (((1,), (1,)), ((), ()))
 
@@ -90,10 +90,10 @@
     sent,
     send1,
     recv1,
+    send2,
+    recv2,
     pair_n,
     recv_n,
-    scan_hot,
-    vox_hot,
     world,
     send_a,
     recv_a,
@@ -130,7 +130,9 @@
     step = SHARE * parts
     arrived = n_map * step
     couples = n_map // 2 * parts
-    message = step * TILE
+    message = parts * 16
+    rest_rows = parts * 8
+    in_plane = n_map * parts
     n_size = pair_n.shape[0] // SHARE
     a_rows = 2 * n_tm
     a_size = SHARE * halves * a_rows
@@ -206,6 +208,7 @@
     turn_of = (
         lax.broadcasted_iota(jnp.int32, (arrived, LANES), 1) // slots + per * lax.rem(chunk_of, parts)
     )
+    top = lax.broadcasted_iota(jnp.int32, (8, LANES), 0) < 4
     own_turn = [turn_of == t for t in range(n_tm)]
     sent[...] = jnp.zeros_like(sent)
 
@@ -215,21 +218,23 @@
     for g in range(spread):
         pose_pad[0:6, g * own_scans : (g + 1) * own_scans] = pose_in[...]
     pose = pose_pad[...]
-    cos, sin = jnp.cos(pose), jnp.sin(pose)
+    cos, sin = jnp.cos(0.5 * pose), jnp.sin(0.5 * pose)
     cx, cy, cz = cos[0:1], cos[1:2], cos[2:3]
     sx, sy, sz = sin[0:1], sin[1:2], sin[2:3]
     pose_rows = [
-        [cz * cy, cz * sy * sx - sz * cx, cz * sy * cx + sz * sx],
-        [sz * cy, sz * sy * sx + cz * cx, sz * sy * cx - cz * sx],
-        [-sy, cy * sx, cy * cx],
-        [pose[3:4], pose[4:5], pose[5:6]],
+        [
+            cx * cy * cz + sx * sy * sz,
+            sx * cy * cz - cx * sy * sz,
+            cx * sy * cz + sx * cy * sz,
+            cx * cy * sz - sx * sy * cz,
+        ],
+        [pose[3:4], pose[4:5], pose[5:6], pose[6:7]],
     ]
     scan_group = lane[0:1] // own_scans
     pose_lines = []
-    for q in range(3):
-        line = pose_rows[0][q]
-        for g in range(1, 4):
-            line = jnp.where(scan_group == g, pose_rows[g][q], line)
+    for line, *others_of in pose_rows:
+        for g, row in enumerate(others_of):
+            line = jnp.where(scan_group == g + 1, row, line)
         pose_lines.append(line)
 
     ids = vox_in[...]
@@ -237,8 +242,8 @@
     lane_of = lax.broadcasted_iota(jnp.int32, ids.shape, 1)
     owner_of = row_of * per + lane_of // slots
     local_ids = jnp.where(ids >= 0, ids - owner_of * voxels, -1).astype(f32)
-    sent[pl.ds(VOX_ROW, chunks, stride=TILE), :] = local_ids
-    sent[pl.ds(SCAN_ROW, chunks, stride=TILE), :] = scan_in[...].astype(f32)
+    sent[pl.ds(8 + VOX_ROW, chunks, stride=16), :] = local_ids
+    sent[pl.ds(8 + SCAN_ROW, chunks, stride=16), :] = scan_in[...].astype(f32)
 
     theta, phi = angle_in[0:1, :], angle_in[1:2, :]
     sin_theta = jnp.sin(theta)
@@ -255,7 +260,7 @@
         sums = [jnp.sum(x, axis=0, keepdims=True) for x in xyz]
         sums += [jnp.sum(xyz[i] * xyz[j], axis=0, keepdims=True) for i, j in PAIRS]
         for k, row in enumerate(sums):
-            sent[pl.ds(r * TILE + k, 1), :] = row
+            sent[pl.ds(r * 16 + (k if k < 8 else 8 + LAST_ROW), 1), :] = row
 
     def load_step(r):
         points_copy(r).wait()
@@ -266,23 +271,27 @@
     row_chunks = n_map // per
 
     def pack(peer_row):
-        for g in range(per):
-            peer = peer_row * per + g
-            for u in range(parts):
+        for u in range(parts):
+            turned = []
+            for g in range(per):
                 for half in range(2):
-                    pieces = [
-                        sent[
-                            aligned(
-                                ((u * per + a) * row_chunks + peer_row) * TILE + 8 * half, 8
-                            ),
-                            :,
-                        ]
-                        for a in range(per)
-                    ]
-                    at = aligned((peer * parts + u) * TILE + 8 * half, 8)
-                    send1[at, :] = group_turn(pieces, g, group, slots)
-            for q in range(3):
-                send1[pl.ds(peer * parts * TILE + POSE_ROW + q, 1), :] = pose_lines[q]
+                    at = [((u * per + a) * row_chunks + peer_row) * 16 + 8 * half for a in range(per)]
+                    pieces = [sent[aligned(row, 8), :] for row in at]
+                    turned.append(group_turn(pieces, g, group, slots))
+            for i in range(per // SHARE):
+                moments, marks, moments_b, marks_b = turned[4 * i : 4 * i + 4]
+                base = (peer_row * (per // SHARE) + i) * parts + u
+                send1[aligned(base * 16 + MARKS, 8), :] = jnp.where(
+                    top, marks, pltpu.roll(marks_b, 4, 0)
+                )
+                send1[aligned(base * 16 + FIRSTS, 8), :] = jnp.where(
+                    top, moments, pltpu.roll(moments_b, 4, 0)
+                )
+                send2[aligned(base * 8, 8), :] = jnp.where(
+                    top, pltpu.roll(moments, 4, 0), moments_b
+                )
+                for k in range(SHARE):
+                    send1[pl.ds(base * 16 + MARKS + 4 * k + POSE_ROW, 1), :] = pose_lines[k]
 
     loop(row_chunks, pack)
 
@@ -290,8 +299,13 @@
     pl.semaphore_wait(barrier, jnp.where(reduces, from_plane, reducers + tm))
     mine = aligned(mp * message, message)
 
-    def message_of(other):
-        return send1.at[aligned(other * message, message), :]
+    rest_mine = aligned(mp * rest_rows, rest_rows)
+
+    def send_moments(other, peer):
+        send(send1.at[aligned(other * message, message), :], recv1.at[mine, :], peer, 0)
+
+    def send_rest(other, peer):
+        send(send2.at[aligned(other * rest_rows, rest_rows), :], recv2.at[rest_mine, :], peer, 8)
 
     def normals_to(t, k):
         return recv_n.at[aligned((t * SHARE + k) * n_size, n_size), :]
@@ -306,12 +320,13 @@
 
         send(pair_n.at[n_mine, :], pair_n.at[n_mine, :], near, 6)
 
-    for other in others:
-        send(message_of(other), recv1.at[mine, :], (tm, other * SHARE + SHARE - 1), 0)
-
-    @pl.when(jnp.logical_not(reduces))
-    def _():
-        send(message_of(rd), recv1.at[mine, :], near, 0)
+    for send_part in (send_moments, send_rest):
+        for other in others:
+            send_part(other, (tm, other * SHARE + SHARE - 1))
+
+        @pl.when(jnp.logical_not(reduces))
+        def _(send_part=send_part):
+            send_part(rd, near)
 
     eight = aligned(rd * 8, 8)
 
@@ -327,6 +342,7 @@
 
         n_column = aligned(tm * SHARE * n_size, SHARE * n_size)
         recv1[mine, :] = send1[aligned(rd * message, message), :]
+        recv2[rest_mine, :] = send2[aligned(rd * rest_rows, rest_rows), :]
         recv_n[n_column, :] = pair_n[...]
         for t in range(n_tm):
             world[pl.ds(3 * n_tm + t, arrived, stride=4 * n_tm), :] = jnp.where(
@@ -336,54 +352,45 @@
         late[...] = jnp.zeros_like(late)
         wait_rows((n_map - 1) * message, recvs.at[0])
 
-        def chunk(k, q, side):
+        def place(q, side):
             i, u = (q // parts, q % parts) if isinstance(q, int) else (q // parts, lax.rem(q, parts))
-            return ((2 * i + side) * SHARE + k) * parts + u
-
-        def couple_row(k, q, row):
+            return (2 * i + side) * parts + u
+
+        def couple_row(k, q, row, turn):
             return jnp.concatenate(
-                [recv1[pl.ds(chunk(k, q, side) * TILE + row, 1), :] for side in range(2)], axis=1
+                [
+                    recv1[pl.ds(place(q, side) * 16 + 4 * k + row + turn, 1), :]
+                    for side in range(2)
+                ],
+                axis=1,
             )
 
         def couple_tile(ref, k, q, rows):
             return jnp.concatenate(
-                [ref[aligned(chunk(k, q, side) * rows, rows), :] for side in range(2)], axis=1
+                [ref[aligned((k * in_plane + place(q, side)) * rows, rows), :] for side in range(2)],
+                axis=1,
             )
 
-        def each_couple(body):
-            for k in range(SHARE):
-                loop(couples, functools.partial(body, k))
-
-        scan_iota = lax.broadcasted_iota(jnp.int32, (scans, 2 * LANES), 0).astype(f32)
-        vox_iota = lax.broadcasted_iota(jnp.int32, (voxels, 2 * LANES), 0).astype(f32)
-
-        def mark_scans(k, q):
-            scan_hot[k * couples + q] = jnp.where(
-                couple_row(k, q, SCAN_ROW) == scan_iota, 1.0, 0.0
-            ).astype(bf16)
-
-        def mark_voxels(k, q):
-            vox_hot[k * couples + q] = jnp.where(
-                couple_row(k, q, VOX_ROW) == vox_iota, 1.0, 0.0
-            ).astype(bf16)
-
-        top = lax.broadcasted_iota(jnp.int32, (8, LANES), 0) < 4
+        def marked(row, count):
+            kind = bf16 if count <= 256 else f32
+            line = jnp.broadcast_to(row, (16, 2 * LANES)).astype(kind)
+            number = lax.broadcasted_iota(jnp.int32, (count, 2 * LANES), 0).astype(f32).astype(kind)
+            found = jnp.concatenate([line] * (count // 16), axis=0) == number
+            return jnp.where(found, jnp.ones((), kind), jnp.zeros((), kind)).astype(bf16)
+
+        again = jnp.minimum(tm, 0)
+
+        def scan_hot(k, q, turn):
+            return marked(couple_row(k, q, SCAN_ROW, turn), scans)
+
+        def vox_hot(k, q, turn):
+            return marked(couple_row(k, q, VOX_ROW, turn), voxels)
+
         own_group = lane // own_scans
-        columns = []
-        for h in range(wide):
-            at = [(h * spread + a) * message + 8 for a in range(spread)]
-            tiles = [recv1[row : row + 8, :] for row in at]
-            turned = [group_turn(tiles, g, own_group, own_scans) for g in range(4)]
-            low = jnp.where(top, pltpu.roll(turned[1], 4, 0), turned[0])
-            high = jnp.where(top, pltpu.roll(turned[3], 4, 0), turned[2])
-            columns.append(jnp.concatenate([low, high], axis=0))
-        table_row = {}
-        for q in range(3):
-            table_row[(1, q)], table_row[(0, q)] = q, 4 + q
-            table_row[(3, q)], table_row[(2, q)] = 8 + q, 12 + q
-
-        def whole_row(row, count):
-            return jnp.broadcast_to(row, (count, LANES))
+        def each_part(ref, row, stride):
+            return jnp.concatenate(
+                [every(ref, row + 4 * k, stride, in_plane) for k in range(SHARE)], axis=0
+            )
 
         def gather(tables, high, low):
             value = jnp.take_along_axis(tables[0], low, axis=1, mode="promise_in_bounds")
@@ -392,17 +399,29 @@
                 value = jnp.where(high == h, other, value)
             return value
 
-        scan_of = every(recv1, SCAN_ROW, TILE).astype(jnp.int32)
+        columns = []
+        for h in range(wide):
+            at = [(h * spread + a) * message + MARKS for a in range(spread)]
+            tiles = [recv1[row : row + 8, :] for row in at]
+            columns.append([group_turn(tiles, g, own_group, own_scans) for g in range(4)])
+        scan_of = each_part(recv1, MARKS + SCAN_ROW, 16).astype(jnp.int32)
         scan_low, scan_high = jnp.bitwise_and(scan_of, LANES - 1), scan_of // LANES
 
-        def pose_of(i, j):
-            row = table_row[(i, j)]
-            rows = [whole_row(tile[row : row + 1], arrived) for tile in columns]
+        def pose_of(k, g):
+            row = 4 * k + POSE_ROW
+            rows = [
+                jnp.broadcast_to(turned[g][row : row + 1], (arrived, LANES)) for turned in columns
+            ]
             return gather(rows, scan_high, scan_low)
 
-        rot = [[pose_of(i, j) for j in range(3)] for i in range(3)]
-        shift = [pose_of(3, j) for j in range(3)]
-        first = [every(recv1, k, TILE) for k in range(3)]
+        qw, qx, qy, qz = [pose_of(0, g) for g in range(4)]
+        shift = [pose_of(1, g) for g in range(3)]
+        rot = [
+            [1 - 2 * (qy * qy + qz * qz), 2 * (qx * qy - qw * qz), 2 * (qx * qz + qw * qy)],
+            [2 * (qx * qy + qw * qz), 1 - 2 * (qx * qx + qz * qz), 2 * (qy * qz - qw * qx)],
+            [2 * (qx * qz - qw * qy), 2 * (qy * qz + qw * qx), 1 - 2 * (qx * qx + qy * qy)],
+        ]
+        first = [each_part(recv1, FIRSTS + k, 16) for k in range(3)]
         turned_first = [sum(rot[i][j] * first[j] for j in range(3)) for i in range(3)]
         m1 = [turned_first[i] + npoints * shift[i] for i in range(3)]
         for c in range(3):
@@ -411,20 +430,18 @@
                     own_turn[t], m1[c], 0.0
                 )
 
-        each_couple(mark_voxels)
-
-        def voxel_sums(ref, rows, k):
+        def voxel_sums(ref, rows, k, turn):
             def add(q):
                 return lax.dot_general(
                     split(couple_tile(ref, k, q, rows)),
-                    vox_hot[k * couples + q],
+                    vox_hot(k, q, turn),
                     CONTRACT_LAST,
                     preferred_element_type=f32,
                 )
 
             return joined(summed(couples, add, 3 * rows, voxels))
 
-        sums = [voxel_sums(world, 4 * n_tm, k) for k in range(SHARE)]
+        sums = [voxel_sums(world, 4 * n_tm, k, 0) for k in range(SHARE)]
         wait_rows((n_tm - 1) * SHARE * n_size, recvs.at[1])
         normal = [
             [
@@ -453,22 +470,18 @@
             send(send_a, recv_a.at[a_mine, :], peer, 2)
         recv_a[a_mine, :] = send_a[...]
 
-        each_couple(mark_scans)
-        vox_of = every(recv1, VOX_ROW, TILE).astype(jnp.int32)
+        vox_of = each_part(recv1, MARKS + VOX_ROW, 16).astype(jnp.int32)
         live = vox_of >= 0
         vox_low = jnp.bitwise_and(vox_of, LANES - 1)
         vox_high = jnp.where(live, vox_of, 0) // LANES
-        part_of = lax.rem(lax.broadcasted_iota(jnp.int32, (step, LANES), 0) // parts, SHARE)
 
         def by_voxel(rows):
             value = None
             for t in range(n_tm):
                 tables = []
                 for h in range(halves):
-                    tab = whole_row(rows(0, t, h), step)
-                    for k in range(1, SHARE):
-                        tab = jnp.where(part_of == k, whole_row(rows(k, t, h), step), tab)
-                    tables.append(jnp.concatenate([tab] * n_map, axis=0))
+                    each = [jnp.broadcast_to(rows(k, t, h), (in_plane, LANES)) for k in range(SHARE)]
+                    tables.append(jnp.concatenate(each, axis=0))
                 found = gather(tables, vox_high, vox_low)
                 value = found if t == 0 else jnp.where(own_turn[t], found, value)
             return value
@@ -479,7 +492,10 @@
                 lambda k, t, h: normal[k][c][t : t + 1, h * LANES : (h + 1) * LANES]
             )
             n.append(jnp.where(live, value, 0.0))
-        second = [every(recv1, 3 + k, TILE) for k in range(6)]
+        wait_rows((n_map - 1) * rest_rows, recvs.at[8])
+        second = [each_part(recv1, FIRSTS + 3, 16)]
+        second += [each_part(recv2, k, 8) for k in range(4)]
+        second += [each_part(recv1, MARKS + LAST_ROW, 16)]
         half_turned = [
             [sum(rot[i][k] * second[PAIR_ROW[(k, j)]] for k in range(3)) for j in range(3)]
             for i in range(3)
@@ -496,7 +512,7 @@
         for t in range(n_tm):
             quads[pl.ds(t, arrived, stride=8), :] = jnp.where(own_turn[t], quad, 0.0)
         for k in range(SHARE):
-            quad_sums = voxel_sums(quads, 8, k)
+            quad_sums = voxel_sums(quads, 8, k, again)
             for t in range(n_tm):
                 for h in range(halves):
                     send_q[t, k * halves + h : k * halves + h + 1, :] = quad_sums[
@@ -535,11 +551,11 @@
         for k in range(len(found), 32):
             terms[pl.ds(k, arrived, stride=32), :] = jnp.zeros_like(rest)
 
-        def scan_sums(k, tile, rows):
+        def scan_sums(k, tile, rows, turn):
             def add(q):
                 return lax.dot_general(
                     split(tile(k, q)),
-                    scan_hot[k * couples + q],
+                    scan_hot(k, q, turn),
                     CONTRACT_LAST,
                     preferred_element_type=f32,
                 )
@@ -547,7 +563,9 @@
             return summed(couples, add, 3 * rows, scans)
 
         per_scan = scale * joined(
-            sum(scan_sums(k, lambda k, q: couple_tile(terms, k, q, 32), 32) for k in range(SHARE))
+            sum(
+                scan_sums(k, lambda k, q: couple_tile(terms, k, q, 32), 32, 0) for k in range(SHARE)
+            )
         )
         for h in range(wide):
             pieces = [per_scan[8 * c : 8 * c + 8, h * LANES : (h + 1) * LANES] for c in range(4)]
@@ -577,7 +595,10 @@
         for i in range(6):
             late[pl.ds(i, arrived, stride=8), :] = shares[i] * offset_of
         moved = scale * joined(
-            sum(scan_sums(k, lambda k, q: couple_tile(late, k, q, 8), 8) for k in range(SHARE))
+            sum(
+                scan_sums(k, lambda k, q: couple_tile(late, k, q, 8), 8, again)
+                for k in range(SHARE)
+            )
         )
         for h in range(wide):
             send_g[h * 8 : h * 8 + 8, :] = moved[:, h * LANES : (h + 1) * LANES]
@@ -646,13 +667,13 @@
 
         @pl.when(jnp.logical_and(reduces, tm == t))
         def _(t=t):
-            rows = (reducers - 1) * message + (n_map - 1) * 16 + halves
+            rows = (reducers - 1) * (message + rest_rows) + (n_map - 1) * 16 + halves
             rows += (n_tm - 1) * (n_size + a_size + SHARE * halves) + (n_tm - 1 - t) * n_size
             wait_rows(rows, sends.at[0])
 
         @pl.when(jnp.logical_and(jnp.logical_not(reduces), tm == t))
         def _(t=t):
-            wait_rows(reducers * message + (t + 1) * n_size, sends.at[0])
+            wait_rows(reducers * (message + rest_rows) + (t + 1) * n_size, sends.at[0])
 
 
 def finish(hess_in, grad_in, cost_in, hess_out, grad_out, cost_out, sems):
@@ -679,14 +700,15 @@
     assert npoints == LANES and slots * 4 == LANES and own_scans * 4 == LANES
     assert n_map % 4 == 0 and n_map % SHARE == 0 and n_tm % 4 == 0 and vox_count % LANES == 0
     scale = own_scans * devices / (blocks * devices * npoints)
-    f32, bf16 = jnp.float32, jnp.bfloat16
+    f32 = jnp.float32
     scans = own_scans * n_map
     halves = vox_count // LANES
-    sent_rows = n_map * n_tm // 4 * TILE
+    in_plane = n_map * n_tm // 4
+    reducers = n_map // SHARE
+    packed = reducers * n_tm // 4
     arrived = SHARE * n_map * n_tm // 4
     n_rows = -(-3 * halves // 8) * 8
     a_rows = SHARE * 2 * n_tm * halves
-    reducers = n_map // SHARE
     hbm = pl.BlockSpec(memory_space=pl.ANY)
     vmem = pl.BlockSpec(memory_space=pltpu.VMEM)
     shapes = [(own_scans, 36), (6, own_scans), (1, vox_count)]
@@ -702,13 +724,13 @@
             pltpu.VMEM((chunks, LANES), jnp.int32),
             pltpu.VMEM((chunks, LANES), jnp.int32),
             pltpu.VMEM((8, LANES), f32),
-            pltpu.VMEM((chunks * TILE, LANES), f32),
-            pltpu.VMEM((sent_rows, LANES), f32),
-            pltpu.VMEM((arrived * TILE, LANES), f32),
+            pltpu.VMEM((chunks * 16, LANES), f32),
+            pltpu.VMEM((packed * 16, LANES), f32),
+            pltpu.VMEM((in_plane * 16, LANES), f32),
+            pltpu.VMEM((packed * 8, LANES), f32),
+            pltpu.VMEM((in_plane * 8, LANES), f32),
             pltpu.VMEM((SHARE * n_rows, LANES), f32),
             pltpu.VMEM((n_tm * SHARE * n_rows, LANES), f32),
-            pltpu.VMEM((arrived // 2, scans, 2 * LANES), bf16),
-            pltpu.VMEM((arrived // 2, vox_count, 2 * LANES), bf16),
             pltpu.VMEM((arrived * 4 * n_tm, LANES), f32),
             pltpu.VMEM((a_rows, LANES), f32),
             pltpu.VMEM((n_tm * a_rows, LANES), f32),
@@ -725,10 +747,10 @@
             pltpu.VMEM((scans // LANES * 8, LANES), f32),
             pltpu.VMEM((reducers * 8, LANES), f32),
             pltpu.VMEM((LANES, LANES), f32),
-            pltpu.SemaphoreType.DMA((4,)),
+            pltpu.SemaphoreType.DMA((2,)),
             pltpu.SemaphoreType.DMA((4,)),
             pltpu.SemaphoreType.DMA((1,)),
-            pltpu.SemaphoreType.DMA((8,)),
+            pltpu.SemaphoreType.DMA((9,)),
         ],
         compiler_params=pltpu.CompilerParams(collective_id=0, has_side_effects=True),
     )(

time: 16.7 us -> 16.4 us (0.982)
  Pallas kernels: 15.9 us -> 15.5 us
    pallas_call x1, Pallas kernels: 15.3 us -> 14.9 us  [local(): pl.pallas_call(functools.partial(kernel, (n_tm, n_map, slots, float(npoin...]
where the time goes in v5:
time: 16.4 us; the launch traced here: 16.2 us
  Pallas kernels  15.5 us (95%)
  between operations  0.64 us (4%)
    pallas_call x1, Pallas kernels, local(): pl.pallas_call(functools.partial(kernel, (n_tm, n_map, slots, float(npoin...  14.9 us
    pallas_call x1, Pallas kernels, local(): pl.pallas_call(finish, out_shape=tuple((jax.ShapeDtypeStruct(shape, f32)...  0.64 us

profile of v5, /device:TPU:0, one launch (start us, length us, event | category | flops | bytes accessed | tf_op | source)
XLA Modules:
  0.0 16.2 jit_solution(1436672801261073853)
XLA Ops:
  0.6 14.9 %shard_map.76 = (f32[32,36]{1,0:T(8,128)S(1)}, f32[6,32]{1,0:T(8,128)S(1)}, f32[1,256]{1,0:T(1,128)S(1)}) custom-call(f32[3,1024,128]{2,1,0:T(8,128)} %points.1, f32[6,32]{1,0:T(8,128)} %poses.1, f32[2,256]{1,0:T(2,128)} %angles.1, s32[8,128]{1,0:T(8,128)} %bitcast.4, s32[8,128]{1,0:T(8,128)} %bitcast.5), custom_call_target="tpu_custom_call" | custom-call | tf_op jit(solution)/shard_map/pallas_call | solution.py:715
  15.5 0.6 %shard_map.77 = (f32[32,36]{1,0:T(8,128)}, f32[6,32]{1,0:T(8,128)}, f32[1,256]{1,0:T(1,128)}) custom-call(f32[32,36]{1,0:T(8,128)S(1)} %get-tuple-element.9.hess_in, f32[6,32]{1,0:T(8,128)S(1)} %get-tuple-element.10.grad_in, f32[1,256]{1,0:T(1,128)S(1)} %get-tuple-element.11.cost_in), custom_call_target="tpu_custom_call" | custom-call | tf_op jit(solution)/shard_map/pallas_call | solution.py:763

commit v6 on v5

--- a/solution.py
+++ b/solution.py
@@ -20,6 +20,7 @@
 MARKS, FIRSTS = 0, 8
 VOX_ROW, SCAN_ROW, LAST_ROW, POSE_ROW = 0, 1, 2, 3
 SHARE = 2
+LEVELS = 4
 CONTRACT_LAST = (((1,), (1,)), ((), ()))
 
 
@@ -134,6 +135,7 @@
     rest_rows = parts * 8
     in_plane = n_map * parts
     n_size = pair_n.shape[0] // SHARE
+    in_level = n_map // LEVELS
     a_rows = 2 * n_tm
     a_size = SHARE * halves * a_rows
     tm = lax.axis_index("tm")
@@ -349,6 +351,7 @@
                 own_turn[t], 1.0, 0.0
             )
         quads[...] = jnp.zeros_like(quads)
+        send_g[...] = jnp.zeros_like(send_g)
         late[...] = jnp.zeros_like(late)
         wait_rows((n_map - 1) * message, recvs.at[0])
 
@@ -377,6 +380,32 @@
             number = lax.broadcasted_iota(jnp.int32, (count, 2 * LANES), 0).astype(f32).astype(kind)
             found = jnp.concatenate([line] * (count // 16), axis=0) == number
             return jnp.where(found, jnp.ones((), kind), jnp.zeros((), kind)).astype(bf16)
+
+        def two_level(values, row, levels, count):
+            low = count // levels
+            number = row.astype(jnp.int32)
+            high_line = jnp.broadcast_to(number // low, (16, 2 * LANES)).astype(f32).astype(bf16)
+            low_row = jnp.bitwise_and(number, low - 1).astype(f32)
+            three = split(values)
+            rows = three.shape[0]
+            high = jnp.concatenate([high_line] * (-(-rows // 16)), axis=0)[:rows]
+            picked = [
+                jnp.where(high == jnp.full((), h, bf16), three, jnp.zeros((), bf16))
+                for h in range(levels)
+            ]
+            return jnp.concatenate(picked, axis=0), marked(low_row, low)
+
+        def product(left, right):
+            return lax.dot_general(left, right, CONTRACT_LAST, preferred_element_type=f32)
+
+        def products(each_side, kinds, rows, columns):
+            if couples > 8:
+                return sum(
+                    summed(couples, lambda q, k=k: product(*each_side(k, q)), rows, columns)
+                    for k in kinds
+                )
+            sides = [each_side(k, q) for k in kinds for q in range(couples)]
+            return product(*[jnp.concatenate(side, axis=1) for side in zip(*sides)])
 
         again = jnp.minimum(tm, 0)
 
@@ -441,7 +470,19 @@
 
             return joined(summed(couples, add, 3 * rows, voxels))
 
-        sums = [voxel_sums(world, 4 * n_tm, k, 0) for k in range(SHARE)]
+        def first_sums(k):
+            rows = 12 * n_tm
+
+            def sides(k, q):
+                values = couple_tile(world, k, q, 4 * n_tm)
+                return two_level(values, couple_row(k, q, VOX_ROW, 0), halves, voxels)
+
+            found = products(sides, [k], halves * rows, LANES)
+            return jnp.concatenate(
+                [joined(found[h * rows : (h + 1) * rows]) for h in range(halves)], axis=1
+            )
+
+        sums = [first_sums(k) for k in range(SHARE)]
         wait_rows((n_tm - 1) * SHARE * n_size, recvs.at[1])
         normal = [
             [
@@ -594,18 +635,20 @@
         offset_of = by_voxel(lambda k, t, h: offset_rows[k][h][t : t + 1])
         for i in range(6):
             late[pl.ds(i, arrived, stride=8), :] = shares[i] * offset_of
-        moved = scale * joined(
-            sum(
-                scan_sums(k, lambda k, q: couple_tile(late, k, q, 8), 8, again)
-                for k in range(SHARE)
+
+        def late_sides(k, q):
+            values = couple_tile(late, k, q, 8)
+            return two_level(values, couple_row(k, q, SCAN_ROW, again), LEVELS, scans)
+
+        moved = products(late_sides, range(SHARE), LEVELS * 24, scans // LEVELS)
+        for h in range(LEVELS):
+            send_g[h * 8 : h * 8 + 8, 0 : scans // LEVELS] = scale * joined(
+                moved[h * 24 : h * 24 + 24]
             )
-        )
-        for h in range(wide):
-            send_g[h * 8 : h * 8 + 8, :] = moved[:, h * LANES : (h + 1) * LANES]
         for peer in plane:
-            source = send_g.at[aligned(peer[1] // spread * 8, 8), :]
+            source = send_g.at[aligned(peer[1] // in_level * 8, 8), :]
             send(source, recv_g.at[eight, :], peer, 5)
-        recv_g[eight, :] = send_g[aligned(mp // spread * 8, 8), :]
+        recv_g[eight, :] = send_g[aligned(mp // in_level * 8, 8), :]
 
         pltpu.make_async_copy(
             recv_q.at[pl.ds(0, n_tm - 1)], recv_q.at[pl.ds(0, n_tm - 1)], recvs.at[3]
@@ -660,7 +703,7 @@
     change = recv_g[0:8, :]
     for m in range(1, reducers):
         change = change + recv_g[m * 8 : m * 8 + 8, :]
-    change = pltpu.roll(change, LANES - own_scans * lax.rem(mp, spread), 1)
+    change = pltpu.roll(change, LANES - own_scans * lax.rem(mp, in_level), 1)
     grad_out[...] = (gradient - change[0:6])[:, 0:own_scans]
 
     for t in range(n_tm):
@@ -698,7 +741,7 @@
     vox_count = normal_angles.shape[1]
     own_scans = poses.shape[1]
     assert npoints == LANES and slots * 4 == LANES and own_scans * 4 == LANES
-    assert n_map % 4 == 0 and n_map % SHARE == 0 and n_tm % 4 == 0 and vox_count % LANES == 0
+    assert n_map % LEVELS == 0 and n_map <= 4 * LEVELS and n_map % 4 == 0 and n_map % SHARE == 0 and n_tm % 4 == 0 and vox_count % LANES == 0
     scale = own_scans * devices / (blocks * devices * npoints)
     f32 = jnp.float32
     scans = own_scans * n_map
@@ -744,7 +787,7 @@
             pltpu.VMEM((arrived * 8, LANES), f32),
             pltpu.VMEM((n_map * 8, LANES), f32),
             pltpu.VMEM((reducers * 8, LANES), f32),
-            pltpu.VMEM((scans // LANES * 8, LANES), f32),
+            pltpu.VMEM((LEVELS * 8, LANES), f32),
             pltpu.VMEM((reducers * 8, LANES), f32),
             pltpu.VMEM((LANES, LANES), f32),
             pltpu.SemaphoreType.DMA((2,)),

time: 16.4 us -> 16 us (0.976)
  Pallas kernels: 15.5 us -> 15.2 us
    pallas_call x1, Pallas kernels: 14.9 us -> 14.6 us  [local(): pl.pallas_call(functools.partial(kernel, (n_tm, n_map, slots, float(npoin...]
where the time goes in v6:
time: 16 us; the launch traced here: 15.8 us
  Pallas kernels  15.2 us (95%)
  between operations  0.64 us (4%)
    pallas_call x1, Pallas kernels, local(): pl.pallas_call(functools.partial(kernel, (n_tm, n_map, slots, float(npoin...  14.6 us
    pallas_call x1, Pallas kernels, local(): pl.pallas_call(finish, out_shape=tuple((jax.ShapeDtypeStruct(shape, f32)...  0.64 us

profile of v6, /device:TPU:0, one launch (start us, length us, event | category | flops | bytes accessed | tf_op | source)
XLA Modules:
  0.0 15.8 jit_solution(4478888957076317171)
XLA Ops:
  0.6 14.6 %shard_map.76 = (f32[32,36]{1,0:T(8,128)S(1)}, f32[6,32]{1,0:T(8,128)S(1)}, f32[1,256]{1,0:T(1,128)S(1)}) custom-call(f32[3,1024,128]{2,1,0:T(8,128)} %points.1, f32[6,32]{1,0:T(8,128)} %poses.1, f32[2,256]{1,0:T(2,128)} %angles.1, s32[8,128]{1,0:T(8,128)} %bitcast.4, s32[8,128]{1,0:T(8,128)} %bitcast.5), custom_call_target="tpu_custom_call" | custom-call | tf_op jit(solution)/shard_map/pallas_call | solution.py:758
  15.2 0.6 %shard_map.77 = (f32[32,36]{1,0:T(8,128)}, f32[6,32]{1,0:T(8,128)}, f32[1,256]{1,0:T(1,128)}) custom-call(f32[32,36]{1,0:T(8,128)S(1)} %get-tuple-element.9.hess_in, f32[6,32]{1,0:T(8,128)S(1)} %get-tuple-element.10.grad_in, f32[1,256]{1,0:T(1,128)S(1)} %get-tuple-element.11.cost_in), custom_call_target="tpu_custom_call" | custom-call | tf_op jit(solution)/shard_map/pallas_call | solution.py:806

commit v7 on v6

--- a/solution.py
+++ b/solution.py
@@ -64,6 +64,13 @@
             acc = acc + body(i)
         return acc
     return lax.fori_loop(0, count, lambda i, total: total + body(i), acc)
+
+
+def flipped(place, bits):
+    for b in range(bits.bit_length()):
+        if bits >> b & 1:
+            place = place + (1 - 2 * lax.rem(place // 2**b, 2)) * 2**b
+    return place
 
 
 def aligned(start, size, unit=8):
@@ -106,6 +113,8 @@
     recv_c,
     terms,
     late,
+    late_high,
+    late_low,
     send_h,
     recv_h,
     send_g,
@@ -164,9 +173,9 @@
     barrier = pltpu.get_barrier_semaphore()
     near = (tm, rd * SHARE + SHARE - 1)
     first_of = (tm, rd * SHARE)
-    plane = [(tm, lax.rem(mp + i, n_map)) for i in range(1, n_map)]
+    plane = [(tm, flipped(mp, i)) for i in range(n_map - 1, 0, -1)]
     column = [(lax.rem(tm + i, n_tm), mp) for i in range(1, n_tm)]
-    others = [lax.rem(rd + i, reducers) for i in range(1, reducers)]
+    others = [flipped(rd, i) for i in range(reducers - 1, 0, -1)]
 
     def greet(peer):
         pl.semaphore_signal(barrier, inc=1, device_id=peer, device_id_type=MESH)
@@ -307,7 +316,7 @@
         send(send1.at[aligned(other * message, message), :], recv1.at[mine, :], peer, 0)
 
     def send_rest(other, peer):
-        send(send2.at[aligned(other * rest_rows, rest_rows), :], recv2.at[rest_mine, :], peer, 8)
+        send(send2.at[aligned(other * rest_rows, rest_rows), :], recv2.at[rest_mine, :], peer, 7)
 
     def normals_to(t, k):
         return recv_n.at[aligned((t * SHARE + k) * n_size, n_size), :]
@@ -381,19 +390,27 @@
             found = jnp.concatenate([line] * (count // 16), axis=0) == number
             return jnp.where(found, jnp.ones((), kind), jnp.zeros((), kind)).astype(bf16)
 
-        def two_level(values, row, levels, count):
+        def two_levels_of(row, levels, count):
             low = count // levels
             number = row.astype(jnp.int32)
-            high_line = jnp.broadcast_to(number // low, (16, 2 * LANES)).astype(f32).astype(bf16)
-            low_row = jnp.bitwise_and(number, low - 1).astype(f32)
+            high = jnp.broadcast_to(number // low, (16, 2 * LANES)).astype(f32).astype(bf16)
+            return high, marked(jnp.bitwise_and(number, low - 1).astype(f32), low)
+
+        def picked(values, high_line, levels):
             three = split(values)
             rows = three.shape[0]
             high = jnp.concatenate([high_line] * (-(-rows // 16)), axis=0)[:rows]
-            picked = [
-                jnp.where(high == jnp.full((), h, bf16), three, jnp.zeros((), bf16))
-                for h in range(levels)
-            ]
-            return jnp.concatenate(picked, axis=0), marked(low_row, low)
+            return jnp.concatenate(
+                [
+                    jnp.where(high == jnp.full((), h, bf16), three, jnp.zeros((), bf16))
+                    for h in range(levels)
+                ],
+                axis=0,
+            )
+
+        def two_level(values, row, levels, count):
+            high, low_marks = two_levels_of(row, levels, count)
+            return picked(values, high, levels), low_marks
 
         def product(left, right):
             return lax.dot_general(left, right, CONTRACT_LAST, preferred_element_type=f32)
@@ -533,7 +550,7 @@
                 lambda k, t, h: normal[k][c][t : t + 1, h * LANES : (h + 1) * LANES]
             )
             n.append(jnp.where(live, value, 0.0))
-        wait_rows((n_map - 1) * rest_rows, recvs.at[8])
+        wait_rows((n_map - 1) * rest_rows, recvs.at[7])
         second = [each_part(recv1, FIRSTS + 3, 16)]
         second += [each_part(recv2, k, 8) for k in range(4)]
         second += [each_part(recv1, MARKS + LAST_ROW, 16)]
@@ -617,6 +634,16 @@
             send(send_h.at[aligned(peer[1] * 8, 8), :], recv_h.at[eight, :], peer, 4)
         recv_h[eight, :] = send_h[aligned(mp * 8, 8), :]
 
+        for k in range(SHARE):
+
+            def keep_marks(q, k=k):
+                at = k * couples + q
+                late_high[at], late_low[at] = two_levels_of(
+                    couple_row(k, q, SCAN_ROW, again), LEVELS, scans
+                )
+
+            loop(couples, keep_marks)
+
         wait_rows((n_tm - 1) * a_size, recvs.at[2])
         offset_rows = []
         for k in range(SHARE):
@@ -637,8 +664,8 @@
             late[pl.ds(i, arrived, stride=8), :] = shares[i] * offset_of
 
         def late_sides(k, q):
-            values = couple_tile(late, k, q, 8)
-            return two_level(values, couple_row(k, q, SCAN_ROW, again), LEVELS, scans)
+            at = k * couples + q + again
+            return picked(couple_tile(late, k, q, 8), late_high[at], LEVELS), late_low[at]
 
         moved = products(late_sides, range(SHARE), LEVELS * 24, scans // LEVELS)
         for h in range(LEVELS):
@@ -660,7 +687,7 @@
         own_floor = total_a[pl.ds(n_tm + tm, SHARE * halves, stride=a_rows), :]
         cost = quad_total / own_floor - own_offset**2
         send_c[...] = cost[0:halves]
-        send(send_c, recv_c, first_of, 7)
+        send(send_c, recv_c, first_of, 6)
         recv_c[...] = cost[halves:]
 
     pl.when(reduces)(reduce_part)
@@ -694,7 +721,7 @@
 
     @pl.when(jnp.logical_not(reduces))
     def _():
-        pltpu.make_async_copy(recv_c, recv_c, recvs.at[7]).wait()
+        pltpu.make_async_copy(recv_c, recv_c, recvs.at[6]).wait()
 
     for h in range(halves):
         cost_out[:, h * LANES : (h + 1) * LANES] = recv_c[h : h + 1, :]
@@ -741,9 +768,9 @@
     vox_count = normal_angles.shape[1]
     own_scans = poses.shape[1]
     assert npoints == LANES and slots * 4 == LANES and own_scans * 4 == LANES
-    assert n_map % LEVELS == 0 and n_map <= 4 * LEVELS and n_map % 4 == 0 and n_map % SHARE == 0 and n_tm % 4 == 0 and vox_count % LANES == 0
+    assert n_map & (n_map - 1) == 0 and n_map % LEVELS == 0 and n_map <= 4 * LEVELS and n_map % 4 == 0 and n_map % SHARE == 0 and n_tm % 4 == 0 and vox_count % LANES == 0
     scale = own_scans * devices / (blocks * devices * npoints)
-    f32 = jnp.float32
+    f32, bf16 = jnp.float32, jnp.bfloat16
     scans = own_scans * n_map
     halves = vox_count // LANES
     in_plane = n_map * n_tm // 4
@@ -785,6 +812,8 @@
             pltpu.VMEM((halves, LANES), f32),
             pltpu.VMEM((arrived * 32, LANES), f32),
             pltpu.VMEM((arrived * 8, LANES), f32),
+            pltpu.VMEM((arrived // 2, 16, 2 * LANES), bf16),
+            pltpu.VMEM((arrived // 2, scans // LEVELS, 2 * LANES), bf16),
             pltpu.VMEM((n_map * 8, LANES), f32),
             pltpu.VMEM((reducers * 8, LANES), f32),
             pltpu.VMEM((LEVELS * 8, LANES), f32),
@@ -793,7 +822,7 @@
             pltpu.SemaphoreType.DMA((2,)),
             pltpu.SemaphoreType.DMA((4,)),
             pltpu.SemaphoreType.DMA((1,)),
-            pltpu.SemaphoreType.DMA((9,)),
+            pltpu.SemaphoreType.DMA((8,)),
         ],
         compiler_params=pltpu.CompilerParams(collective_id=0, has_side_effects=True),
     )(

time: 16 us -> 15.9 us (level)
  no operation moved by 1% of the time
where the time goes in v7:
time: 15.9 us; the launch traced here: 15.7 us
  Pallas kernels  15.1 us (95%)
  between operations  0.64 us (4%)
    pallas_call x1, Pallas kernels, local(): pl.pallas_call(functools.partial(kernel, (n_tm, n_map, slots, float(npoin...  14.5 us
    pallas_call x1, Pallas kernels, local(): pl.pallas_call(finish, out_shape=tuple((jax.ShapeDtypeStruct(shape, f32)...  0.64 us

profile of v7, /device:TPU:0, one launch (start us, length us, event | category | flops | bytes accessed | tf_op | source)
XLA Modules:
  0.0 15.7 jit_solution(5892814171417949311)
XLA Ops:
  0.6 14.5 %shard_map.76 = (f32[32,36]{1,0:T(8,128)S(1)}, f32[6,32]{1,0:T(8,128)S(1)}, f32[1,256]{1,0:T(1,128)S(1)}) custom-call(f32[3,1024,128]{2,1,0:T(8,128)} %points.1, f32[6,32]{1,0:T(8,128)} %poses.1, f32[2,256]{1,0:T(2,128)} %angles.1, s32[8,128]{1,0:T(8,128)} %bitcast.4, s32[8,128]{1,0:T(8,128)} %bitcast.5), custom_call_target="tpu_custom_call" | custom-call | tf_op jit(solution)/shard_map/pallas_call | solution.py:785
  15.1 0.6 %shard_map.77 = (f32[32,36]{1,0:T(8,128)}, f32[6,32]{1,0:T(8,128)}, f32[1,256]{1,0:T(1,128)}) custom-call(f32[32,36]{1,0:T(8,128)S(1)} %get-tuple-element.9.hess_in, f32[6,32]{1,0:T(8,128)S(1)} %get-tuple-element.10.grad_in, f32[1,256]{1,0:T(1,128)S(1)} %get-tuple-element.11.cost_in), custom_call_target="tpu_custom_call" | custom-call | tf_op jit(solution)/shard_map/pallas_call | solution.py:835

commit v8 on v7

--- a/solution.py
+++ b/solution.py
@@ -18,7 +18,7 @@
 ROWS = [("h", i, j) for i in range(6) for j in range(i, 6)] + [("g", i) for i in range(6)]
 
 MARKS, FIRSTS = 0, 8
-VOX_ROW, SCAN_ROW, LAST_ROW, POSE_ROW = 0, 1, 2, 3
+VOX_ROW, SCAN_ROW, POSE_ROW = 0, 1, 3
 SHARE = 2
 LEVELS = 4
 CONTRACT_LAST = (((1,), (1,)), ((), ()))
@@ -96,6 +96,7 @@
     scan_in,
     pose_pad,
     sent,
+    sent2,
     send1,
     recv1,
     send2,
@@ -141,7 +142,7 @@
     arrived = n_map * step
     couples = n_map // 2 * parts
     message = parts * 16
-    rest_rows = parts * 8
+    rest_rows = step * 8
     in_plane = n_map * parts
     n_size = pair_n.shape[0] // SHARE
     in_level = n_map // LEVELS
@@ -222,6 +223,7 @@
     top = lax.broadcasted_iota(jnp.int32, (8, LANES), 0) < 4
     own_turn = [turn_of == t for t in range(n_tm)]
     sent[...] = jnp.zeros_like(sent)
+    sent2[...] = jnp.zeros_like(sent2)
 
     for copy in small:
         copy.wait()
@@ -253,8 +255,8 @@
     lane_of = lax.broadcasted_iota(jnp.int32, ids.shape, 1)
     owner_of = row_of * per + lane_of // slots
     local_ids = jnp.where(ids >= 0, ids - owner_of * voxels, -1).astype(f32)
-    sent[pl.ds(8 + VOX_ROW, chunks, stride=16), :] = local_ids
-    sent[pl.ds(8 + SCAN_ROW, chunks, stride=16), :] = scan_in[...].astype(f32)
+    sent[pl.ds(4 + VOX_ROW, chunks, stride=8), :] = local_ids
+    sent[pl.ds(4 + SCAN_ROW, chunks, stride=8), :] = scan_in[...].astype(f32)
 
     theta, phi = angle_in[0:1, :], angle_in[1:2, :]
     sin_theta = jnp.sin(theta)
@@ -265,44 +267,48 @@
             k = part * n_size + c * halves + h
             pair_n[pl.ds(k, 1), :] = own_normal[c][:, h * LANES : (h + 1) * LANES]
 
-    def raw_moments(r):
+    def first_moments(r):
         at = aligned(r * LANES, LANES, LANES)
-        xyz = [pts[i, at, :].T for i in range(3)]
-        sums = [jnp.sum(x, axis=0, keepdims=True) for x in xyz]
-        sums += [jnp.sum(xyz[i] * xyz[j], axis=0, keepdims=True) for i, j in PAIRS]
-        for k, row in enumerate(sums):
-            sent[pl.ds(r * 16 + (k if k < 8 else 8 + LAST_ROW), 1), :] = row
+        for i in range(3):
+            turned = pts[i, at, :].T
+            pts[i, at, :] = turned
+            sent[pl.ds(r * 8 + i, 1), :] = jnp.sum(turned, axis=0, keepdims=True)
+
+    def second_moments(r):
+        at = aligned(r * LANES, LANES, LANES)
+        xyz = [pts[i, at, :] for i in range(3)]
+        for k, (i, j) in enumerate(PAIRS):
+            sent2[pl.ds(r * 8 + k, 1), :] = jnp.sum(xyz[i] * xyz[j], axis=0, keepdims=True)
 
     def load_step(r):
         points_copy(r).wait()
         for i in range(span // LANES):
-            raw_moments(r * (span // LANES) + i)
+            first_moments(r * (span // LANES) + i)
 
     loop(loads, load_step)
     row_chunks = n_map // per
 
+    def turned_tiles(ref, peer_row, u):
+        at = [((u * per + a) * row_chunks + peer_row) * 8 for a in range(per)]
+        pieces = [ref[aligned(row, 8), :] for row in at]
+        return [group_turn(pieces, g, group, slots) for g in range(per)]
+
     def pack(peer_row):
         for u in range(parts):
-            turned = []
-            for g in range(per):
-                for half in range(2):
-                    at = [((u * per + a) * row_chunks + peer_row) * 16 + 8 * half for a in range(per)]
-                    pieces = [sent[aligned(row, 8), :] for row in at]
-                    turned.append(group_turn(pieces, g, group, slots))
+            tiles = turned_tiles(sent, peer_row, u)
             for i in range(per // SHARE):
-                moments, marks, moments_b, marks_b = turned[4 * i : 4 * i + 4]
-                base = (peer_row * (per // SHARE) + i) * parts + u
-                send1[aligned(base * 16 + MARKS, 8), :] = jnp.where(
-                    top, marks, pltpu.roll(marks_b, 4, 0)
-                )
-                send1[aligned(base * 16 + FIRSTS, 8), :] = jnp.where(
-                    top, moments, pltpu.roll(moments_b, 4, 0)
-                )
-                send2[aligned(base * 8, 8), :] = jnp.where(
-                    top, pltpu.roll(moments, 4, 0), moments_b
-                )
+                low, high = tiles[SHARE * i : SHARE * (i + 1)]
+                base = ((peer_row * (per // SHARE) + i) * parts + u) * 16
+                send1[aligned(base + FIRSTS, 8), :] = jnp.where(top, low, pltpu.roll(high, 4, 0))
+                send1[aligned(base + MARKS, 8), :] = jnp.where(top, pltpu.roll(low, 4, 0), high)
                 for k in range(SHARE):
-                    send1[pl.ds(base * 16 + MARKS + 4 * k + POSE_ROW, 1), :] = pose_lines[k]
+                    send1[pl.ds(base + MARKS + 4 * k + POSE_ROW, 1), :] = pose_lines[k]
+
+    def pack_rest(peer_row):
+        for u in range(parts):
+            for g, tile in enumerate(turned_tiles(sent2, peer_row, u)):
+                base = (peer_row * (per // SHARE) + g // SHARE) * parts + u
+                send2[aligned((base * SHARE + g % SHARE) * 8, 8), :] = tile
 
     loop(row_chunks, pack)
 
@@ -331,19 +337,27 @@
 
         send(pair_n.at[n_mine, :], pair_n.at[n_mine, :], near, 6)
 
-    for send_part in (send_moments, send_rest):
+    def to_reducers(send_part):
         for other in others:
             send_part(other, (tm, other * SHARE + SHARE - 1))
 
         @pl.when(jnp.logical_not(reduces))
-        def _(send_part=send_part):
+        def _():
             send_part(rd, near)
 
-    eight = aligned(rd * 8, 8)
-
-    def reduce_part():
+    to_reducers(send_moments)
+
+    @pl.when(reduces)
+    def _():
         for peer in column:
             send(pair_n.at[pl.ds(n_size, n_size), :], normals_to(tm, 1), peer, 1)
+
+    loop(chunks, second_moments)
+    loop(row_chunks, pack_rest)
+    to_reducers(send_rest)
+    eight = aligned(rd * 8, 8)
+
+    def reduce_part():
         wait_rows(n_size, recvs.at[6])
         for peer in column:
 
@@ -433,9 +447,9 @@
             return marked(couple_row(k, q, VOX_ROW, turn), voxels)
 
         own_group = lane // own_scans
-        def each_part(ref, row, stride):
+        def each_part(ref, row, gap):
             return jnp.concatenate(
-                [every(ref, row + 4 * k, stride, in_plane) for k in range(SHARE)], axis=0
+                [every(ref, row + gap * k, 16, in_plane) for k in range(SHARE)], axis=0
             )
 
         def gather(tables, high, low):
@@ -450,7 +464,7 @@
             at = [(h * spread + a) * message + MARKS for a in range(spread)]
             tiles = [recv1[row : row + 8, :] for row in at]
             columns.append([group_turn(tiles, g, own_group, own_scans) for g in range(4)])
-        scan_of = each_part(recv1, MARKS + SCAN_ROW, 16).astype(jnp.int32)
+        scan_of = each_part(recv1, MARKS + SCAN_ROW, 4).astype(jnp.int32)
         scan_low, scan_high = jnp.bitwise_and(scan_of, LANES - 1), scan_of // LANES
 
         def pose_of(k, g):
@@ -467,7 +481,7 @@
             [2 * (qx * qy + qw * qz), 1 - 2 * (qx * qx + qz * qz), 2 * (qy * qz - qw * qx)],
             [2 * (qx * qz - qw * qy), 2 * (qy * qz + qw * qx), 1 - 2 * (qx * qx + qy * qy)],
         ]
-        first = [each_part(recv1, FIRSTS + k, 16) for k in range(3)]
+        first = [each_part(recv1, FIRSTS + k, 4) for k in range(3)]
         turned_first = [sum(rot[i][j] * first[j] for j in range(3)) for i in range(3)]
         m1 = [turned_first[i] + npoints * shift[i] for i in range(3)]
         for c in range(3):
@@ -528,7 +542,7 @@
             send(send_a, recv_a.at[a_mine, :], peer, 2)
         recv_a[a_mine, :] = send_a[...]
 
-        vox_of = each_part(recv1, MARKS + VOX_ROW, 16).astype(jnp.int32)
+        vox_of = each_part(recv1, MARKS + VOX_ROW, 4).astype(jnp.int32)
         live = vox_of >= 0
         vox_low = jnp.bitwise_and(vox_of, LANES - 1)
         vox_high = jnp.where(live, vox_of, 0) // LANES
@@ -551,9 +565,7 @@
             )
             n.append(jnp.where(live, value, 0.0))
         wait_rows((n_map - 1) * rest_rows, recvs.at[7])
-        second = [each_part(recv1, FIRSTS + 3, 16)]
-        second += [each_part(recv2, k, 8) for k in range(4)]
-        second += [each_part(recv1, MARKS + LAST_ROW, 16)]
+        second = [each_part(recv2, k, 8) for k in range(6)]
         half_turned = [
             [sum(rot[i][k] * second[PAIR_ROW[(k, j)]] for k in range(3)) for j in range(3)]
             for i in range(3)
@@ -794,11 +806,12 @@
             pltpu.VMEM((chunks, LANES), jnp.int32),
             pltpu.VMEM((chunks, LANES), jnp.int32),
             pltpu.VMEM((8, LANES), f32),
-            pltpu.VMEM((chunks * 16, LANES), f32),
+            pltpu.VMEM((chunks * 8, LANES), f32),
+            pltpu.VMEM((chunks * 8, LANES), f32),
             pltpu.VMEM((packed * 16, LANES), f32),
             pltpu.VMEM((in_plane * 16, LANES), f32),
-            pltpu.VMEM((packed * 8, LANES), f32),
-            pltpu.VMEM((in_plane * 8, LANES), f32),
+            pltpu.VMEM((packed * 16, LANES), f32),
+            pltpu.VMEM((in_plane * 16, LANES), f32),
             pltpu.VMEM((SHARE * n_rows, LANES), f32),
             pltpu.VMEM((n_tm * SHARE * n_rows, LANES), f32),
             pltpu.VMEM((arrived * 4 * n_tm, LANES), f32),

time: 15.9 us -> 16 us (level)
  no operation moved by 1% of the time
where the time goes in v8:
time: 16 us; the launch traced here: 15.8 us
  Pallas kernels  15.2 us (95%)
  between operations  0.64 us (4%)
    pallas_call x1, Pallas kernels, local(): pl.pallas_call(functools.partial(kernel, (n_tm, n_map, slots, float(npoin...  14.5 us
    pallas_call x1, Pallas kernels, local(): pl.pallas_call(finish, out_shape=tuple((jax.ShapeDtypeStruct(shape, f32)...  0.64 us

profile of v8, /device:TPU:0, one launch (start us, length us, event | category | flops | bytes accessed | tf_op | source)
XLA Modules:
  0.0 15.8 jit_solution(10429746015365079934)
XLA Ops:
  0.6 14.5 %shard_map.76 = (f32[32,36]{1,0:T(8,128)S(1)}, f32[6,32]{1,0:T(8,128)S(1)}, f32[1,256]{1,0:T(1,128)S(1)}) custom-call(f32[3,1024,128]{2,1,0:T(8,128)} %points.1, f32[6,32]{1,0:T(8,128)} %poses.1, f32[2,256]{1,0:T(2,128)} %angles.1, s32[8,128]{1,0:T(8,128)} %bitcast.4, s32[8,128]{1,0:T(8,128)} %bitcast.5), custom_call_target="tpu_custom_call" | custom-call | tf_op jit(solution)/shard_map/pallas_call | solution.py:797
  15.2 0.6 %shard_map.77 = (f32[32,36]{1,0:T(8,128)}, f32[6,32]{1,0:T(8,128)}, f32[1,256]{1,0:T(1,128)}) custom-call(f32[32,36]{1,0:T(8,128)S(1)} %get-tuple-element.9.hess_in, f32[6,32]{1,0:T(8,128)S(1)} %get-tuple-element.10.grad_in, f32[1,256]{1,0:T(1,128)S(1)} %get-tuple-element.11.cost_in), custom_call_target="tpu_custom_call" | custom-call | tf_op jit(solution)/shard_map/pallas_call | solution.py:848
